TPU v7x, 32 devices: a whole 2x2x4 slice. The times are simulated.
32 devices in a mesh: seq: 16 (over z, y, core), batch: 2 (over x).
Axes of the slice: x: 2, y: 2, z: 4, core: 2. Of those that a mesh axis runs over, the one named last changes fastest.
Arguments:
- queries: bfloat16 [4096, 1792], P(('batch', 'seq')), parts along dimension 0, may hold values from -128 to 128
- keys: bfloat16 [4096, 256], P(('batch', 'seq')), parts along dimension 0, may hold values from -4 to 4
- values: bfloat16 [4096, 256], P(('batch', 'seq')), parts along dimension 0, may hold values from -4 to 4
- out_grad: bfloat16 [4096, 1792], P(('batch', 'seq')), parts along dimension 0, may hold values from -24 to 24
- row_delta: float32 [4096, 14], P(('batch', 'seq')), parts along dimension 0, may hold values from -6 to 6
- layer_input: bfloat16 [4096, 3584], P(('batch', 'seq')), parts along dimension 0, may hold values from -6 to 6
- norm_gain: float32 [3584], replicated, may hold values from 0.25 to 1.75
- qkv_weight: bfloat16 [3584, 2304], P('seq'), may hold values from -0.5 to 0.5
- block_order: int32 [64], P('batch'), parts along dimension 0, may hold values from 0 to 31, as said below
- block_mask: int32 [64, 32], P('batch'), parts along dimension 0, may hold values from 0 to 1, as said below
- frame_owner: int32 [32], P('batch'), parts along dimension 0, may hold values from 0 to 15, as said below
- vision_features: bfloat16 [32, 128, 1152], P(('batch', 'seq')), parts along dimension 0, may hold values from -6 to 6
- post_gain: float32 [1152], replicated, may hold values from 0.25 to 1.75
- projector: bfloat16 [1152, 3584], replicated, may hold values from -0.1875 to 0.1875
Outputs:
- token_grad: bfloat16 [4096, 3584], P(('batch', 'seq')), parts along dimension 0
- encoder_grad: bfloat16 [32, 128, 1152], P(('batch', 'seq')), parts along dimension 0
There are 2 independent parts, one for each index of `batch`. A program takes and returns all parts, laid end to end along the dimension named above; an argument that names none is the same for every part. Nothing has to cross between parts.
Inputs may be any that keep to these rules, and one draw needn't show every extreme that they name: `block_order`: entries 2i and 2i + 1 are the blocks of device i of seq; all entries together are a permutation; each device's two blocks sum to 31; for every frame f, blocks 2f and 2f + 1 lie on devices 2j and 2j + 1 for some j. `block_mask`: 1 on the diagonal, 0 above it. `frame_owner`: every device of seq owns exactly one frame, and the owner of frame f holds block 2f or block 2f + 1.
All inputs are finite; a program needn't handle non-finite values.
Results may differ from a plain program's by a relative error of at most 0.012.
Values may be sent and summed in bfloat16 or wider, within the bound.
A program may use at most 128 MiB of HBM per device.

v0:
```python
import functools

import jax
import jax.numpy as jnp
from jax import lax
from jax.experimental import pallas as pl
from jax.experimental.pallas import tpu as pltpu
from jax.sharding import PartitionSpec as P

HQ = 14
KVH = 2
HD = 128
GROUP = HQ // KVH
CHUNK = 4
LOG2E = 1.4426950408889634


EPSILON = 1e-06
NEGATIVE = -1e30


def attention_kernel(
    order_ref,
    mask_ref,
    q_hbm,
    do_hbm,
    delta_ref,
    kv_hbm,
    dq_ref,
    dkv_ref,
    slots,
    scores,
    dq_acc,
    acc,
    q_ref,
    do_ref,
    kv_ref,
    load_sem,
):
    loads = [
        pltpu.make_async_copy(source, target, load_sem.at[i])
        for i, (source, target) in enumerate(
            ((kv_hbm, kv_ref), (q_hbm, q_ref), (do_hbm, do_ref))
        )
    ]
    for load in loads:
        load.start()
    me = lax.axis_index("seq")
    blocks = order_ref.shape[0]
    half = q_ref.shape[0] // 2
    lanes = delta_ref.shape[2]
    tall = CHUNK * half
    scaling = HD ** (-0.5)
    factor = scaling * LOG2E
    width = KVH * HD
    acc[...] = jnp.zeros_like(acc)

    row = lax.broadcasted_iota(jnp.int32, (tall, lanes), 0)
    query_at = lax.rem(lax.broadcasted_iota(jnp.int32, (tall, lanes), 1), half)
    ahead = (row < half) & (row > query_at)

    for load in loads:
        load.wait()

    for b in range(2):
        own = 2 * me + b
        query_block = order_ref[own]
        slots[0] = own

        def collect(slot, count):
            key_block = order_ref[slot]
            live = (mask_ref[query_block, key_block] == 1) & (key_block < query_block)
            slots[count] = slot
            return count + live.astype(jnp.int32)

        count = lax.fori_loop(0, blocks, collect, jnp.int32(1))
        for extra in range(CHUNK):
            slots[count + extra] = own
        chunks = (count + CHUNK - 1) // CHUNK

        for g in range(KVH):
            pad = jnp.zeros((lanes - GROUP * half, HD), jnp.bfloat16)

            def stacked(ref):
                parts = [
                    ref[b * half : (b + 1) * half, h * HD : (h + 1) * HD]
                    for h in range(g * GROUP, (g + 1) * GROUP)
                ]
                return jnp.concatenate(parts + [pad], axis=0)

            queries = stacked(q_ref)
            grads = stacked(do_ref)
            delta = delta_ref[2 * g + b]

            def key_rows(chunk, first_col):
                parts = [
                    kv_ref[
                        pl.ds(pl.multiple_of(slots[chunk * CHUNK + i] * half, half), half),
                        first_col : first_col + HD,
                    ]
                    for i in range(CHUNK)
                ]
                return jnp.concatenate(parts, axis=0)

            def score_pass(chunk, top):
                keys = key_rows(chunk, g * HD)
                score = lax.dot_general(
                    keys, queries, (((1,), (1,)), ((), ())), preferred_element_type=jnp.float32
                )
                limit = jnp.minimum((count - chunk * CHUNK) * half, tall)
                dead = (row >= limit) | (ahead & (chunk == 0))
                score = jnp.where(dead, NEGATIVE, score)
                scores[chunk] = score
                return jnp.maximum(top, jnp.max(score.reshape(tall // 8, 8, lanes), axis=0))

            top = lax.fori_loop(
                0, chunks, score_pass, jnp.full((8, lanes), NEGATIVE, jnp.float32)
            )
            top = jnp.max(top, axis=0, keepdims=True)

            def exp_pass(chunk, total):
                spread = jnp.exp2((scores[chunk] - top) * factor)
                scores[chunk] = spread
                return total + jnp.sum(spread.reshape(tall // 8, 8, lanes), axis=0)

            total = lax.fori_loop(0, chunks, exp_pass, jnp.zeros((8, lanes), jnp.float32))
            inverse = 1.0 / jnp.sum(total, axis=0, keepdims=True)
            dq_acc[...] = jnp.zeros_like(dq_acc)

            def grad_pass(chunk, carry):
                keys = key_rows(chunk, g * HD)
                vals = key_rows(chunk, width + g * HD)
                prob = scores[chunk] * inverse
                value_add = jnp.dot(
                    prob.astype(jnp.bfloat16), grads, preferred_element_type=jnp.float32
                )
                prob_grad = lax.dot_general(
                    vals, grads, (((1,), (1,)), ((), ())), preferred_element_type=jnp.float32
                )
                score_grad = (prob * (prob_grad - delta)).astype(jnp.bfloat16)
                key_add = (
                    jnp.dot(score_grad, queries, preferred_element_type=jnp.float32) * scaling
                )
                dq_acc[...] += lax.dot_general(
                    keys, score_grad, (((0,), (0,)), ((), ())), preferred_element_type=jnp.float32
                )
                for i in range(CHUNK):
                    here = pl.ds(pl.multiple_of(slots[chunk * CHUNK + i] * half, half), half)
                    part = slice(i * half, (i + 1) * half)
                    acc[here, g * HD : (g + 1) * HD] += key_add[part]
                    acc[here, width + g * HD : width + (g + 1) * HD] += value_add[part]
                return carry

            lax.fori_loop(0, chunks, grad_pass, 0)
            turned = (jnp.transpose(dq_acc[...]) * scaling).astype(jnp.bfloat16)
            for j in range(GROUP):
                h = g * GROUP + j
                dq_ref[b * half : (b + 1) * half, h * HD : (h + 1) * HD] = turned[
                    j * half : (j + 1) * half
                ]
    dkv_ref[...] = acc[...].astype(dkv_ref.dtype)


def attention_grads(order, mask, queries, out_grad, row_delta, kv):
    rows = queries.shape[0]
    half = rows // 2
    keys = kv.shape[0]
    lanes = -(-GROUP * half // 128) * 128
    blocks = order.shape[0]
    delta = jnp.transpose(row_delta.reshape(2, half, KVH, GROUP), (2, 0, 3, 1))
    delta = delta.reshape(2 * KVH, 1, GROUP * half)
    delta = jnp.pad(delta, ((0, 0), (0, 0), (0, lanes - GROUP * half)))
    max_chunks = -(-blocks // CHUNK)
    smem = pl.BlockSpec(memory_space=pltpu.SMEM)
    vmem = pl.BlockSpec(memory_space=pltpu.VMEM)
    anywhere = pl.BlockSpec(memory_space=pl.ANY)
    return pl.pallas_call(
        attention_kernel,
        out_shape=(
            jax.ShapeDtypeStruct((rows, HQ * HD), jnp.bfloat16),
            jax.ShapeDtypeStruct((keys, 2 * KVH * HD), jnp.bfloat16),
        ),
        in_specs=[smem, smem, anywhere, anywhere, vmem, anywhere],
        out_specs=(vmem, vmem),
        scratch_shapes=[
            pltpu.SMEM((blocks + CHUNK + 1,), jnp.int32),
            pltpu.VMEM((max_chunks, CHUNK * half, lanes), jnp.float32),
            pltpu.VMEM((HD, lanes), jnp.float32),
            pltpu.VMEM((keys, 2 * KVH * HD), jnp.float32),
            pltpu.VMEM(queries.shape, queries.dtype),
            pltpu.VMEM(out_grad.shape, out_grad.dtype),
            pltpu.VMEM(kv.shape, kv.dtype),
            pltpu.SemaphoreType.DMA((3,)),
        ],
        cost_estimate=pl.CostEstimate(
            flops=5 * rows * keys * HQ * HD,
            bytes_accessed=4 * keys * KVH * HD * 2 + 3 * rows * HQ * HD * 2,
            transcendentals=rows * keys * HQ // 2,
        ),
        compiler_params=pltpu.CompilerParams(vmem_limit_bytes=67043328),
        name="attention_grads",
    )(order, mask, queries, out_grad, delta, kv)


MESH = pl.DeviceIdType.MESH


def remote(src, dst, send_sem, recv_sem, device):
    return pltpu.make_async_remote_copy(
        src_ref=src,
        dst_ref=dst,
        send_sem=send_sem,
        recv_sem=recv_sem,
        device_id=device,
        device_id_type=MESH,
    )


def when(condition, action):
    if condition is None:
        action()
    else:
        pl.when(condition)(action)


def places():
    me = lax.axis_index("seq")
    x = lax.rem(lax.axis_index("batch"), 2)
    z, y, c = me // 4, lax.rem(me // 2, 2), lax.rem(me, 2)
    return me, x, z, y, c


def gather_kernel(
    depth,
    k_ref,
    v_ref,
    w_ref,
    kv_all,
    w_all,
    kv_own,
    w_own,
    own_sem,
    kv_recv,
    kv_core_recv,
    kv_up,
    kv_down,
    kv_y,
    kv_core,
    w_recv,
    w_x_recv,
    w_core_recv,
    w_up,
    w_down,
    w_y,
    w_x,
    w_core,
):
    me, x, z, y, c = places()
    rows = w_ref.shape[0]
    width = k_ref.shape[1]
    part = 5 * (rows // 16) // 14 * 16
    up, down = {"seq": me + 4}, {"seq": me - 4}
    beside, core = {"seq": me + 2 - 4 * y}, {"seq": me + 1 - 2 * c}
    across = {"batch": lax.axis_index("batch") + 1 - 2 * x}
    has_up, has_down = z < depth - 1, z > 0

    loads = [
        pltpu.make_async_copy(k_ref, kv_own.at[:, 0:width], own_sem.at[0]),
        pltpu.make_async_copy(v_ref, kv_own.at[:, width : 2 * width], own_sem.at[1]),
        pltpu.make_async_copy(w_ref, w_own, own_sem.at[2]),
    ]
    for load in loads:
        load.start()
    barrier = pltpu.get_barrier_semaphore()
    for peer, present in (
        (up, has_up),
        (down, has_down),
        (beside, None),
        (core, None),
        (across, None),
    ):
        when(
            present,
            lambda peer=peer: pl.semaphore_signal(
                barrier, inc=1, device_id=peer, device_id_type=MESH
            ),
        )
    pl.semaphore_wait(barrier, 3 + has_up.astype(jnp.int32) + has_down.astype(jnp.int32))
    for load in loads:
        load.wait()

    started = []

    def start(copy, condition=None):
        when(condition, copy.start)
        started.append((condition, copy))

    def both(first, second):
        return second if first is None else jnp.logical_and(first, second)

    def line(step):
        if step == 0:
            return [(z, None, None)]
        return [(z - step, z - step >= 0, True), (z + step, z + step < depth, False)]

    def safe(j):
        return jnp.clip(j, 0, depth - 1)

    def slot(j, side):
        return 2 * j + side

    def arrived(ref, semaphore, condition=None):
        when(condition, remote(ref, ref, own_sem.at[3], semaphore, core).wait_recv)

    own_kv = pltpu.make_async_copy(kv_own, kv_all.at[me], own_sem.at[4])
    own_w = pltpu.make_async_copy(w_own, w_all.at[me], own_sem.at[5])

    def kv_at(u):
        return kv_all.at[2 * u + c]

    def kv_core_pass(src, u, condition):
        start(remote(src, kv_at(u), kv_core.at[u], kv_core_recv.at[u], core), condition)

    def kv_pass(j, condition, upward):
        u = slot(j, y)
        src = kv_own if upward is None else kv_at(u)
        if upward is not False:
            start(remote(src, kv_at(u), kv_up.at[j], kv_recv.at[u], up), both(condition, has_up))
        if upward is not True:
            start(
                remote(src, kv_at(u), kv_down.at[j], kv_recv.at[u], down),
                both(condition, has_down),
            )
        start(remote(src, kv_at(u), kv_y.at[j], kv_recv.at[u], beside), condition)
        kv_core_pass(src, u, condition)

    spans = [
        pl.ds(pl.multiple_of(x * (rows - part), 16), part),
        pl.ds(part, rows - 2 * part),
        pl.ds(pl.multiple_of((1 - x) * (rows - part), 16), part),
    ]

    def w_at(u, r):
        return w_all.at[2 * u + c, spans[r]]

    def w_core_pass(src, u, r, condition):
        start(remote(src, w_at(u, r), w_core.at[r, u], w_core_recv.at[r, u], core), condition)

    def w_share(u, r, condition):
        if r == 0:
            start(
                remote(w_at(u, 0), w_at(u, 0), w_x.at[u], w_x_recv.at[u], across), condition
            )
        w_core_pass(w_at(u, r), u, r, condition)

    def w_pass(j, r, condition, upward):
        u = slot(j, y)
        src = w_own.at[spans[r]] if upward is None else w_at(u, r)
        dst = w_at(u, r)
        if upward is not False:
            start(remote(src, dst, w_up.at[r, j], w_recv.at[r, u], up), both(condition, has_up))
        if upward is not True:
            start(
                remote(src, dst, w_down.at[r, j], w_recv.at[r, u], down),
                both(condition, has_down),
            )
        start(remote(src, dst, w_y.at[r, j], w_recv.at[r, u], beside), condition)

    kv_pass(z, None, None)
    for r in (0, 1):
        w_pass(z, r, None, None)
    for r in (0, 1, 2):
        w_core_pass(w_own.at[spans[r]], slot(z, y), r, None)
    own_kv.start()
    own_w.start()

    waiting = []
    for step in range(1, depth + 1):
        shared = []
        ahead = [(safe(j), present, upward) for j, present, upward in line(step)]
        ahead = ahead if step < depth else []
        aside = [(slot(safe(j), 1 - y), present) for j, present, _ in line(step - 1)]
        for j, condition, upward in ahead:
            arrived(kv_at(slot(j, y)), kv_recv.at[slot(j, y)], condition)
            kv_pass(j, condition, upward)
        for u, condition in aside:
            arrived(kv_at(u), kv_recv.at[u], condition)
            kv_core_pass(kv_at(u), u, condition)
        for r in (0, 1):
            for j, condition, upward in ahead:
                u = slot(j, y)
                arrived(w_at(u, r), w_recv.at[r, u], condition)
                w_pass(j, r, condition, upward)
                w_share(u, r, condition)
            for u, condition in aside:
                arrived(w_at(u, r), w_recv.at[r, u], condition)
                w_share(u, r, condition)
        shared = [(slot(j, y), condition) for j, condition, _ in ahead] + aside
        for u, condition in waiting:
            arrived(w_at(u, 2), w_x_recv.at[u], condition)
            w_core_pass(w_at(u, 2), u, 2, condition)
        waiting = shared
    for u, condition in waiting:
        arrived(w_at(u, 2), w_x_recv.at[u], condition)
        w_core_pass(w_at(u, 2), u, 2, condition)

    for u in range(2 * depth):
        from_core = 2 * u + 1 - c
        arrived(kv_all.at[from_core], kv_core_recv.at[u])
        for r in (0, 1, 2):
            arrived(w_all.at[from_core, spans[r]], w_core_recv.at[r, u])
    for condition, copy in started:
        when(condition, copy.wait_send)
    own_kv.wait()
    own_w.wait()


def gather(keys, values, weight, count):
    depth = count // 4
    kv_shape = (keys.shape[0], 2 * keys.shape[1])

    def sems(*shape):
        return pltpu.SemaphoreType.DMA(shape)

    pairs = 2 * depth
    anywhere = pl.BlockSpec(memory_space=pl.ANY)
    return pl.pallas_call(
        functools.partial(gather_kernel, depth),
        out_shape=(
            jax.ShapeDtypeStruct((count,) + kv_shape, keys.dtype),
            jax.ShapeDtypeStruct((count,) + weight.shape, weight.dtype),
        ),
        in_specs=[anywhere, anywhere, anywhere],
        out_specs=(anywhere, anywhere),
        scratch_shapes=[
            pltpu.VMEM(kv_shape, keys.dtype),
            pltpu.VMEM(weight.shape, weight.dtype),
            sems(6),
            sems(pairs),
            sems(pairs),
            sems(depth),
            sems(depth),
            sems(depth),
            sems(pairs),
            sems(2, pairs),
            sems(pairs),
            sems(3, pairs),
            sems(2, depth),
            sems(2, depth),
            sems(2, depth),
            sems(pairs),
            sems(3, pairs),
        ],
        compiler_params=pltpu.CompilerParams(collective_id=0, has_side_effects=True),
        name="gather",
    )(keys, values, weight)


def reduce_kernel(
    depth,
    part_ref,
    out_ref,
    core_in,
    sum_out,
    y_in,
    z_in,
    core_send,
    core_recv,
    y_send,
    y_recv,
    z_send,
    z_recv,
):
    me, x, z, y, c = places()
    beside, core = {"seq": me + 2 - 4 * y}, {"seq": me + 1 - 2 * c}

    def far(k):
        return lax.rem(z + k, depth)

    barrier = pltpu.get_barrier_semaphore()
    peers = [beside, core] + [{"seq": 4 * far(k) + 2 * y + c} for k in range(1, depth)]
    for peer in peers:
        pl.semaphore_signal(barrier, inc=1, device_id=peer, device_id_type=MESH)
    pl.semaphore_wait(barrier, len(peers))

    def wide(ref):
        return ref[...].astype(jnp.float32)

    order = list(range(1, depth)) + [0]
    started = []

    def start(copy):
        copy.start()
        started.append(copy)

    core_copies, y_copies = {}, {}
    for side in (1, 0):
        for k in order:
            u = 2 * far(k) + (y if side == 0 else 1 - y)
            copy = remote(
                part_ref.at[2 * u + 1 - c], core_in.at[u], core_send.at[u], core_recv.at[u], core
            )
            start(copy)
            core_copies[side, k] = (copy, u)

    def arrived(ref, send_semaphore, semaphore, device):
        remote(ref, ref, send_semaphore, semaphore, device).wait_recv()

    for k in order:
        j = far(k)
        u = 2 * j + 1 - y
        arrived(core_in.at[u], core_send.at[u], core_recv.at[u], core)
        total = wide(part_ref.at[2 * u + c]) + wide(core_in.at[u])
        sum_out[u] = total.astype(sum_out.dtype)
        start(remote(sum_out.at[u], y_in.at[j], y_send.at[j], y_recv.at[j], beside))
    for k in order:
        j = far(k)
        u = 2 * j + y
        arrived(core_in.at[u], core_send.at[u], core_recv.at[u], core)
        total = wide(part_ref.at[2 * u + c]) + wide(core_in.at[u])
        arrived(y_in.at[j], y_send.at[j], y_recv.at[j], beside)
        total = total + wide(y_in.at[j])
        if k != 0:
            sum_out[u] = total.astype(sum_out.dtype)
            start(
                remote(
                    sum_out.at[u],
                    z_in.at[z],
                    z_send.at[j],
                    z_recv.at[z],
                    {"seq": 4 * j + 2 * y + c},
                )
            )
    for k in range(1, depth):
        j = far(k)
        arrived(z_in.at[j], z_send.at[j], z_recv.at[j], core)
        total = total + wide(z_in.at[j])
    out_ref[...] = total.astype(out_ref.dtype)
    for copy in started:
        copy.wait_send()


def reduce_shards(parts, count):
    depth = count // 4
    block = parts.shape[1:]
    line, pairs = pltpu.SemaphoreType.DMA((depth,)), pltpu.SemaphoreType.DMA((2 * depth,))
    vmem = pl.BlockSpec(memory_space=pltpu.VMEM)
    return pl.pallas_call(
        functools.partial(reduce_kernel, depth),
        out_shape=jax.ShapeDtypeStruct(block, parts.dtype),
        in_specs=[vmem],
        out_specs=vmem,
        scratch_shapes=[
            pltpu.VMEM((2 * depth,) + block, parts.dtype),
            pltpu.VMEM((2 * depth,) + block, parts.dtype),
            pltpu.VMEM((depth,) + block, parts.dtype),
            pltpu.VMEM((depth,) + block, parts.dtype),
            pairs,
            pairs,
            line,
            line,
            line,
            line,
        ],
        compiler_params=pltpu.CompilerParams(collective_id=1, has_side_effects=True),
        name="reduce_shards",
    )(parts)


def swapped(array, axis, apart):
    return lax.ppermute(array, axis, [(i, i ^ 1 << apart) for i in range(lax.axis_size(axis))])


def body(
    queries,
    keys,
    values,
    out_grad,
    row_delta,
    layer_input,
    norm_gain,
    qkv_weight,
    block_order,
    block_mask,
    frame_owner,
    vision_features,
    post_gain,
    projector,
):
    tok_rows = queries.shape[0]
    half_len = tok_rows // 2
    my_index = lax.axis_index("seq")
    my_blocks = lax.dynamic_slice_in_dim(block_order, 2 * my_index, 2, 0)
    count = lax.axis_size("seq")
    kv_all, weight_all = gather(keys, values, qkv_weight, count)
    kv = kv_all.reshape(count * tok_rows, kv_all.shape[2])
    weight = weight_all.reshape(count * qkv_weight.shape[0], qkv_weight.shape[1])
    query_grad, kv_part = attention_grads(
        block_order, block_mask, queries, out_grad, row_delta, kv
    )
    kv_grad = reduce_shards(kv_part.reshape(kv_all.shape), count)
    head_grads = jnp.concatenate([query_grad, kv_grad], axis=1)
    norm_grad = jnp.dot(
        head_grads,
        weight.T,
        preferred_element_type=jnp.float32,
    ).astype(jnp.bfloat16)
    inputs = layer_input.astype(jnp.float32)
    inverse = lax.rsqrt(jnp.mean(inputs * inputs, axis=1, keepdims=True) + EPSILON)
    scaled = norm_grad.astype(jnp.float32) * norm_gain
    token_grad = (
        inverse * scaled - inputs * inverse**3 * jnp.mean(scaled * inputs, axis=1, keepdims=True)
    ).astype(jnp.bfloat16)
    frame_table = jnp.arange(frame_owner.shape[0], dtype=jnp.int32)
    my_frame = jnp.sum(jnp.where(frame_owner == my_index, frame_table, 0))
    keep_first = my_blocks[0] // 2 == my_frame
    kept_block = jnp.where(keep_first, my_blocks[0], my_blocks[1])
    leading = kept_block % 2 == 0
    halves = token_grad.reshape(2, half_len, token_grad.shape[1])
    kept = jnp.where(keep_first, halves[0], halves[1])
    sending = jnp.where(keep_first, halves[1], halves[0])
    received = swapped(sending, "seq", 0)
    frame_rows = jnp.where(
        leading,
        jnp.concatenate([kept, received], axis=0),
        jnp.concatenate([received, kept], axis=0),
    )
    post_grad = jnp.dot(frame_rows, projector.T, preferred_element_type=jnp.float32)
    features = vision_features[0].astype(jnp.float32)
    centered = features - jnp.mean(features, axis=1, keepdims=True)
    deviation = lax.rsqrt(jnp.mean(centered * centered, axis=1, keepdims=True) + EPSILON)
    normed = centered * deviation
    weighted = post_grad * post_gain
    encoder_grad = (
        deviation
        * (
            weighted
            - jnp.mean(weighted, axis=1, keepdims=True)
            - normed * jnp.mean(weighted * normed, axis=1, keepdims=True)
        )
    ).astype(jnp.bfloat16)
    return (token_grad, encoder_grad[None])


def solution(mesh):
    placed = (
        P(("batch", "seq"), None),
        P(("batch", "seq"), None),
        P(("batch", "seq"), None),
        P(("batch", "seq"), None),
        P(("batch", "seq"), None),
        P(("batch", "seq"), None),
        P(),
        P("seq", None),
        P("batch"),
        P("batch", None),
        P("batch"),
        P(("batch", "seq"), None, None),
        P(),
        P(),
    )
    return jax.shard_map(
        body,
        mesh=mesh,
        in_specs=placed,
        out_specs=(P(("batch", "seq"), None), P(("batch", "seq"), None, None)),
        check_vma=False,
    )
```

profile of v0, /device:TPU:0, one launch (start us, length us, event | category | flops | bytes accessed | tf_op | source)
XLA Modules:
  0.0 147.8 jit_solution(595536606614046357)
XLA Ops:
  0.6 0.7 dynamic_slice.3
  1.4 0.6 fusion.31
  4.5 0.8 reshape.65
  5.3 0.1 reshape.70
  5.4 0.6 pad.4.delta_ref
  6.0 79.4 %gather.1 = (bf16[16,128,512]{2,1,0:T(8,128)(2,1)}, bf16[16,224,2304]{2,1,0:T(8,128)(2,1)}) custom-call(bf16[128,256]{1,0:T(8,128)(2,1)} %k_ref.1, bf16[128,256]{1,0:T(8,128)(2,1)} %v_ref.1, bf16[224,2304]{1,0:T(8,128)(2,1)} %w_ref.1), custom_call_target="tpu_custom_call" | custom-call | tf_op jit(solution)/shard_map/gather/pallas_call | solution.py:427
  85.4 13.2 %attention_grads.1 = (bf16[128,1792]{1,0:T(8,128)(2,1)}, bf16[2048,512]{1,0:T(8,128)(2,1)}) custom-call(s32[32]{0:T(128)} %order_ref.1, s32[32,32]{1,0:T(8,128)} %mask_ref.1, bf16[128,1792]{1,0:T(8,128)(2,1)} %q_hbm.1, bf16[128,1792]{1,0:T(8,128)(2,1)} %do_hbm.1, f32[4,1,512]{2,1,0:T(1,128)} %pad.4.delta_ref, bf16[2048,512]{1,0:T(8,128)(2,1)} %bitcast.41), custom_call_target="tpu_custom_call" | custom-call | flops 2348810240 | bytes 5570560 | tf_op jit(solution)/shard_map/attention_grads/pallas_call | solution.py:177
  98.6 0.0 copy-start.6
  98.6 0.0 copy-start.1
  98.6 0.0 copy-start.3
  98.6 0.0 copy-start.4
  98.6 25.0 %reduce_shards.1 = bf16[128,512]{1,0:T(8,128)(2,1)} custom-call(bf16[16,128,512]{2,1,0:T(8,128)(2,1)} %bitcast.39), custom_call_target="tpu_custom_call" | custom-call | tf_op jit(solution)/shard_map/reduce_shards/pallas_call | solution.py:548
  123.7 0.0 copy-done.6
  123.7 0.6 fusion.27
  124.3 0.0 copy-done.1
  124.3 0.0 copy-done.3
  124.3 0.0 copy-done.4
  124.3 11.2 %fusion.2 = (f32[128]{0:T(128)S(1)}, f32[128]{0:T(128)S(1)}, f32[128,3584]{1,0:T(8,128)S(1)}) fusion(bf16[128,3584]{1,0:T(8,128)(2,1)S(1)} %copy-done.1, f32[3584]{0:T(1024)S(1)} %copy-done.4, bf16[3584,2304]{1,0:T(8,128)(2,1)} %bitcast.38, bf16[128,512]{1,0:T(8,128)(2,1)} %reduce_shards.1, bf16[128,1792]{1,0:T(8,128)(2,1)S(1)} %copy-done.3), kind=kOutput, calls=%fused_computation.7 | convolution fusion | flops 2118778624 | bytes 19872768 | tf_op jit(solution)/shard_map/dot_general | solution.py:603
  136.2 1.6 %fusion.5 = bf16[128,3584]{1,0:T(8,128)(2,1)S(1)} fusion(bf16[128,3584]{1,0:T(8,128)(2,1)} %param.19, f32[128,3584]{1,0:T(8,128)S(1)} %get-tuple-element.20, f32[128]{0:T(128)S(1)} %get-tuple-element.22, f32[128]{0:T(128)S(1)} %get-tuple-element.19, f32[128]{0:T(128)S(1)} %get-tuple-element.18), kind=kLoop, calls=%fused_computation.10 | loop fusion | flops 2752512 | bytes 3671552 | tf_op jit(solution)/shard_map/convert_element_type | solution.py:613
  137.9 0.0 copy-start
  137.9 0.0 copy-start.2
  137.9 0.0 copy-start.5
  137.9 0.1 broadcast_select_fusion.1
  138.0 0.1 collective-permute-start
  138.1 1.0 copy-done.2
  139.1 0.1 convert_reduce_fusion
  140.4 0.2 fusion.22
  140.7 0.0 collective-permute-done
  140.7 0.0 copy-done.5
  140.7 6.1 %fusion.30 = (f32[128]{0:T(128)S(1)}, f32[128]{0:T(128)S(1)}, f32[128,1152]{1,0:T(8,128)S(1)}) fusion(f32[128]{0:T(128)S(1)} %add_rsqrt_fusion, f32[128]{0:T(128)S(1)} %broadcast_multiply_fusion.2, bf16[1,128,1152]{2,1,0:T(8,128)(2,1)S(1)} %copy-done.2, f32[1152]{0:T(1024)S(1)} %copy-done.5, bf16[1152,3584]{1,0:T(8,128)(2,1)} %param.27, ...), kind=kOutput, calls=%fused_computation.49 | convolution fusion | flops 1062125312 | bytes 10066433 | tf_op jit(solution)/shard_map/dot_general | solution.py:628
  146.8 0.0 copy-done
  146.9 1.0 fusion.26
  (6 shorter events, 0.0 us)
Async XLA Ops:
  98.6 25.1 %copy-start.6 = (s32[16]{0:T(128)S(1)}, s32[16]{0:T(128)}, u32[]{:S(2)}) copy-start(s32[16]{0:T(128)} %param.24) | copy-start | bytes 196
  98.6 25.7 %copy-start.1 = (bf16[128,3584]{1,0:T(8,128)(2,1)S(1)}, bf16[128,3584]{1,0:T(8,128)(2,1)}, u32[]{:S(2)}) copy-start(bf16[128,3584]{1,0:T(8,128)(2,1)} %param.19) | copy-start | bytes 2752516
  98.6 25.7 %copy-start.3 = (bf16[128,1792]{1,0:T(8,128)(2,1)S(1)}, bf16[128,1792]{1,0:T(8,128)(2,1)}, u32[]{:S(2)}) copy-start(bf16[128,1792]{1,0:T(8,128)(2,1)} %get-tuple-element.7) | copy-start | bytes 1376260
  98.6 25.7 %copy-start.4 = (f32[3584]{0:T(1024)S(1)}, f32[3584]{0:T(1024)}, u32[]{:S(2)}) copy-start(f32[3584]{0:T(1024)} %param.20) | copy-start | bytes 43012
  137.9 9.0 %copy-start = (bf16[128,3584]{1,0:T(8,128)(2,1)}, bf16[128,3584]{1,0:T(8,128)(2,1)S(1)}, u32[]{:S(2)}) copy-start(bf16[128,3584]{1,0:T(8,128)(2,1)S(1)} %fusion.5) | copy-start | bytes 2752516
  137.9 1.2 copy-start.2
  137.9 2.8 %copy-start.5 = (f32[1152]{0:T(1024)S(1)}, f32[1152]{0:T(1024)}, u32[]{:S(2)}) copy-start(f32[1152]{0:T(1024)} %param.26) | copy-start | bytes 13828
  138.0 2.7 %collective-permute-start = (bf16[64,3584]{1,0:T(8,128)(2,1)S(1)}, bf16[64,3584]{1,0:T(8,128)(2,1)S(1)}, u32[]{:S(2)}, u32[]{:S(2)}) collective-permute-start(bf16[64,3584]{1,0:T(8,128)(2,1)S(1)} %get-tuple-element.15), channel_id=1, source_target_pairs={{0,2},{2,0},{4,6},{6,4},{8,10},{10,8},{12,14},{14,12},{16,18},{18,... | collective-permute-start | bytes 1376264 | tf_op jit(solution)/shard_map/ppermute | solution.py:571
where the time goes:
time: 148 us
  Pallas kernels  118 us (80%)
  matrix products  17.4 us (12%)
  between operations  5.28 us (4%)
  local copies, waits for them, and re-layouts  3.86 us (3%)
  other arithmetic  3.68 us (2%)
    pallas_call x1, Pallas kernels, gather(): pl.pallas_call(functools.partial(gather_kernel, depth), out_shape=(jax.Sh...  79.4 us
    pallas_call x1, Pallas kernels, reduce_shards(): pl.pallas_call(functools.partial(reduce_kernel, depth), out_shape=jax.Sha...  25 us
    pallas_call x1, Pallas kernels, attention_grads(): pl.pallas_call(attention_kernel, out_shape=(jax.ShapeDtypeStruct((rows, H...  13.2 us
    dot_general x1, matrix products, body(): jnp.dot(head_grads, weight.T, preferred_element_type=jnp.float32)  11.2 us
    dot_general x1, matrix products, body(): jnp.dot(frame_rows, projector.T, preferred_element_type=jnp.float32)  6.14 us
  transfers between devices with their start and end apart: 1, of which 0 were waited for; matrix products, arithmetic and copies ran while one was open for 0% of the time, Pallas kernels for 0%

commit v1 on v0

v1 whole, which is shorter than its diff:
```python
import functools

import jax
import jax.numpy as jnp
from jax import lax
from jax.experimental import pallas as pl
from jax.experimental.pallas import tpu as pltpu
from jax.sharding import PartitionSpec as P

HQ = 14
KVH = 2
HD = 128
GROUP = HQ // KVH
WIDE = GROUP * HD
LOG2E = 1.4426950408889634
EPSILON = 1e-06
NEGATIVE = -1e30
PIECES = 3
MESH = pl.DeviceIdType.MESH


def when(condition, action):
    if condition is None:
        action()
    else:
        pl.when(condition)(action)


def split_rows(size, count):
    tiles = size // 16
    edges = [tiles * i // count for i in range(count + 1)]
    return [(16 * a, 16 * (b - a)) for a, b in zip(edges, edges[1:]) if b > a]


class Copies:
    def __init__(self, send_sem, recv_sem):
        self.send_sem, self.recv_sem = send_sem, recv_sem
        self.sends, self.recvs = 0, 0
        self.started = []

    def slots(self, count=1):
        self.recvs += count
        return self.recvs - count

    def send(self, src, dst, recv, device, condition=None):
        copy = pltpu.make_async_remote_copy(
            src_ref=src,
            dst_ref=dst,
            send_sem=self.send_sem.at[self.sends],
            recv_sem=self.recv_sem.at[recv],
            device_id=device,
            device_id_type=MESH,
        )
        self.sends += 1
        when(condition, copy.start)
        self.started.append((condition, copy))

    def wait(self, ref, recv, device, condition=None):
        copy = pltpu.make_async_remote_copy(
            src_ref=ref,
            dst_ref=ref,
            send_sem=self.send_sem.at[0],
            recv_sem=self.recv_sem.at[recv],
            device_id=device,
            device_id_type=MESH,
        )
        when(condition, copy.wait_recv)

    def drain(self):
        for condition, copy in self.started:
            when(condition, copy.wait_send)


def layer_kernel(
    depth,
    order_ref,
    mask_ref,
    queries_ref,
    grads_ref,
    delta_hbm,
    keys_ref,
    values_ref,
    weight_ref,
    out_ref,
    k_all,
    v_all,
    q_in,
    g_in,
    d_in,
    w_all,
    k_sort,
    v_sort,
    q_sort,
    g_sort,
    d_sort,
    d_pad,
    scores,
    top,
    total,
    dq_acc,
    acc,
    part,
    core_in,
    sum_out,
    z_in,
    h_q,
    h_kv,
    y_out,
    y_in,
    load_sem,
    send_sem,
    recv_sem,
):
    me = lax.axis_index("seq")
    batch = lax.axis_index("batch")
    x = lax.rem(batch, 2)
    z, y, c = me // 4, lax.rem(me // 2, 2), lax.rem(me, 2)
    rows = q_in.shape[1]
    half = rows // 2
    lanes = 2 * GROUP * half
    shard = weight_ref.shape[0]
    scaling = HD ** (-0.5)
    factor = scaling * LOG2E

    up, down = {"seq": me + 4}, {"seq": me - 4}
    beside, core = {"seq": me + 2 - 4 * y}, {"seq": me + 1 - 2 * c}
    corner = {"seq": me + 2 - 4 * y + 1 - 2 * c}
    across = {"batch": batch + 1 - 2 * x}
    has_up, has_down = z < depth - 1, z > 0

    def far(k):
        return lax.rem(z + k, depth)

    def behind(k):
        return lax.rem(z + depth - k, depth)

    def plane(j):
        return {"seq": 4 * j + 2 * y + c}

    def head_at(ref, side, width):
        return ref.at[:, pl.ds(pl.multiple_of(side * width, 128), width)]

    def load(src, dst, index):
        copy = pltpu.make_async_copy(src, dst, load_sem.at[index])
        copy.start()
        return copy

    load_k = load(head_at(keys_ref, y, HD), k_all.at[z, c, y], 0)
    load_v = load(head_at(values_ref, y, HD), v_all.at[z, c, y], 1)
    load_w = load(weight_ref, w_all.at[z], 2)
    load_q = load(head_at(queries_ref, y, WIDE), q_in.at[y], 3)
    load_g = load(head_at(grads_ref, y, WIDE), g_in.at[y], 4)
    load_d = load(delta_hbm, d_in.at[y], 5)

    barrier = pltpu.get_barrier_semaphore()
    peers = [beside, core, corner, across] + [plane(far(k)) for k in range(1, depth)]
    for peer in peers:
        pl.semaphore_signal(barrier, inc=1, device_id=peer, device_id_type=MESH)
    pl.semaphore_wait(barrier, len(peers))

    copies = Copies(send_sem, recv_sem)

    over_y = copies.slots(5)
    copies.send(head_at(keys_ref, 1 - y, HD), k_all.at[z, c, y], over_y, beside)
    copies.send(head_at(values_ref, 1 - y, HD), v_all.at[z, c, y], over_y + 1, beside)
    copies.send(head_at(queries_ref, 1 - y, WIDE), q_in.at[y], over_y + 2, beside)
    copies.send(head_at(grads_ref, 1 - y, WIDE), g_in.at[y], over_y + 3, beside)
    copies.send(delta_hbm, d_in.at[y], over_y + 4, beside)

    def spread(ref, load_own, swap):
        arrive = copies.slots(2 * depth)
        shared = copies.slots(2)

        def own(side, index):
            for k in range(depth - 1, 0, -1):
                copies.send(
                    ref.at[z, c, side], ref.at[z, c, side], arrive + 2 * k + index, plane(far(k))
                )
            copies.send(ref.at[z, c, side], ref.at[z, c, side], shared + index, core)

        def first():
            load_own.wait()
            own(y, 0)

        def second():
            copies.wait(ref.at[z, c, 1 - y], swap, beside)
            own(1 - y, 1)

        passed = copies.slots(depth)

        def relay():
            for k in range(1, depth):
                j = behind(k)
                for index in range(2):
                    side = y if index == 0 else 1 - y
                    copies.wait(ref.at[j, c, side], arrive + 2 * k + index, core)
                copies.send(ref.at[j, c], ref.at[j, c], passed + k, core)

        def finish():
            for index in range(2):
                side = y if index == 0 else 1 - y
                copies.wait(ref.at[z, 1 - c, side], shared + index, core)
            for k in range(1, depth):
                copies.wait(ref.at[behind(k), 1 - c], passed + k, core)

        return first, second, relay, finish

    k_first, k_second, k_relay, k_finish = spread(k_all, load_k, over_y)
    v_first, v_second, v_relay, v_finish = spread(v_all, load_v, over_y + 1)
    k_first()
    k_second()
    v_first()
    v_second()

    own_part = shard // 32 * 16
    between = shard - 2 * own_part
    pieces = split_rows(own_part, PIECES)

    def w_at(j, side, start, size):
        base = pl.multiple_of(side * (shard - own_part) + start, 16)
        return w_all.at[j, pl.ds(base, size)]

    def w_middle(j):
        return w_all.at[j, pl.ds(own_part, between)]

    count = len(pieces)
    w_recv = [copies.slots(depth) for _ in range(count + 1)]
    w_cross = [copies.slots(depth) for _ in range(count)]

    def w_send(j, upward, downward):
        for i in range(count + (between > 0)):
            ref = w_at(j, x, *pieces[i]) if i < count else w_middle(j)
            if upward is not None:
                copies.send(ref, ref, w_recv[i] + j, up, upward)
            if downward is not None:
                copies.send(ref, ref, w_recv[i] + j, down, downward)

    def w_relay(step):
        for j, present, upward in (
            (z - step, z - step >= 0, True),
            (z + step, z + step < depth, False),
        ):
            at = jnp.clip(j, 0, depth - 1)
            go = jnp.logical_and(present, has_up if upward else has_down)
            for i in range(count + (between > 0)):
                ref = w_at(at, x, *pieces[i]) if i < count else w_middle(at)
                copies.wait(ref, w_recv[i] + at, core, present)
                copies.send(ref, ref, w_recv[i] + at, up if upward else down, go)
                if i < count:
                    copies.send(ref, ref, w_cross[i] + at, across, present)

    def w_finish(j, other):
        for i in range(count):
            copies.wait(w_at(j, 1 - x, *pieces[i]), w_cross[i] + j, across, other)

    load_w.wait()
    w_send(z, has_up, has_down)

    def turned(device):
        return order_ref[2 * device] > order_ref[2 * device + 1]

    def arrange(source, target, side):
        flip = turned(4 * z + 2 * side + c)
        for h in range(GROUP):
            first = source[side, 0:half, h * HD : (h + 1) * HD]
            second = source[side, half:rows, h * HD : (h + 1) * HD]
            at = (side * GROUP + h) * half
            target[0, at : at + half] = jnp.where(flip, second, first)
            target[1, at : at + half] = jnp.where(flip, first, second)

    for copy in (load_q, load_g, load_d):
        copy.wait()
    k_relay()
    copies.wait(q_in.at[1 - y], over_y + 2, beside)
    for side in range(2):
        arrange(q_in, q_sort, side)

    def sort_keys(source, target):
        def one(index, carry):
            j, device = index // 4, lax.rem(index, 4)
            owner, side = device // 2, lax.rem(device, 2)
            flip = turned(4 * j + 2 * side + owner)
            first = source[j, owner, side, 0:half]
            second = source[j, owner, side, half:rows]
            at = pl.ds(pl.multiple_of(device * half, half), half)
            target[0, j, at] = jnp.where(flip, second, first)
            target[1, j, at] = jnp.where(flip, first, second)
            return carry

        lax.fori_loop(0, 4 * depth, one, 0)

    k_finish()
    sort_keys(k_all, k_sort)

    tiles = 3 * depth
    lane = lax.broadcasted_iota(jnp.int32, (1, lanes), 1)
    query_row = lax.rem(lane, half)
    in_first = lane < GROUP * half
    key_row = lax.broadcasted_iota(jnp.int32, (half, lanes), 0)

    def block_of(device, high):
        one, two = order_ref[2 * device], order_ref[2 * device + 1]
        return jnp.where(high == 1, jnp.maximum(one, two), jnp.minimum(one, two))

    def tile(t):
        kind, j = t // depth, lax.rem(t, depth)
        return j, kind // 2, (kind + 1) // 2

    top[...] = jnp.full_like(top, NEGATIVE)
    total[...] = jnp.zeros_like(total)
    acc[...] = jnp.zeros_like(acc)
    dq_acc[...] = jnp.zeros_like(dq_acc)

    def score_pass(t, carry):
        j, key_high, query_high = tile(t)
        score = lax.dot_general(
            k_sort[key_high, j],
            q_sort[query_high],
            (((1,), (1,)), ((), ())),
            preferred_element_type=jnp.float32,
        )
        query_blocks = [block_of(4 * z + 2 * side + c, query_high) for side in range(2)]
        best = top[query_high]
        for device in range(4):
            owner, side = device // 2, device % 2
            key_block = block_of(4 * j + 2 * side + owner, key_high)
            base, slope = [], []
            for query_block in query_blocks:
                live = (mask_ref[query_block, key_block] == 1) & (key_block <= query_block)
                same = live & (key_block == query_block)
                slope.append(same.astype(jnp.int32))
                base.append(jnp.where(same, 0, jnp.where(live, half, -1)))
            limit = jnp.where(in_first, base[0], base[1]) + query_row * jnp.where(
                in_first, slope[0], slope[1]
            )
            slab = score[device * half : (device + 1) * half]
            slab = jnp.where(key_row <= limit, slab, NEGATIVE)
            scores[t, device * half : (device + 1) * half] = slab
            best = jnp.maximum(best, jnp.max(slab.reshape(half // 8, 8, lanes), axis=0))
        top[query_high] = best
        return carry

    lax.fori_loop(0, tiles, score_pass, 0)
    v_relay()
    for high in range(2):
        best = jnp.max(top[high], axis=0, keepdims=True)
        top[high] = jnp.broadcast_to(best * factor, (8, lanes))

    def sum_pass(t, carry):
        j, key_high, query_high = tile(t)
        peak = top[query_high][0:1]
        spread_out = jnp.exp2(scores[t] * factor - peak)
        total[query_high] += jnp.sum(spread_out.reshape(4 * half // 8, 8, lanes), axis=0)
        return carry

    lax.fori_loop(0, tiles, sum_pass, 0)
    for high in range(2):
        whole = jnp.sum(total[high], axis=0, keepdims=True)
        shift = top[high][0:1] + jnp.log2(whole)
        top[high] = jnp.broadcast_to(shift, (8, lanes))

    def spread_rows(line):
        return jnp.broadcast_to(line, (8, line.shape[1]))

    copies.wait(g_in.at[1 - y], over_y + 3, beside)
    copies.wait(d_in.at[1 - y], over_y + 4, beside)
    for side in range(2):
        arrange(g_in, g_sort, side)
        d_pad[...] = jnp.zeros_like(d_pad)
        d_pad[:, 0 : d_in.shape[2]] = d_in[side]
        flipped = jnp.transpose(d_pad[...])
        flip = turned(4 * z + 2 * side + c)
        for h in range(GROUP):
            line = jnp.where(y == 1, flipped[GROUP + h : GROUP + h + 1], flipped[h : h + 1])
            first, second = line[:, 0:half], line[:, half:rows]
            at = (side * GROUP + h) * half
            d_sort[0, :, at : at + half] = spread_rows(jnp.where(flip, second, first))
            d_sort[1, :, at : at + half] = spread_rows(jnp.where(flip, first, second))
    v_finish()
    sort_keys(v_all, v_sort)

    def grad_pass(t, carry):
        j, key_high, query_high = tile(t)
        prob = jnp.exp2(scores[t] * factor - top[query_high][0:1])
        grads = g_sort[query_high]
        prob_grad = lax.dot_general(
            v_sort[key_high, j], grads, (((1,), (1,)), ((), ())), preferred_element_type=jnp.float32
        )
        score_grad = (prob * (prob_grad - d_sort[query_high][0:1])).astype(jnp.bfloat16)
        acc[key_high, j, :, HD : 2 * HD] += jnp.dot(
            prob.astype(jnp.bfloat16), grads, preferred_element_type=jnp.float32
        )
        acc[key_high, j, :, 0:HD] += jnp.dot(
            score_grad, q_sort[query_high], preferred_element_type=jnp.float32
        )
        dq_acc[query_high] += lax.dot_general(
            k_sort[key_high, j],
            score_grad,
            (((0,), (0,)), ((), ())),
            preferred_element_type=jnp.float32,
        )
        return carry

    lax.fori_loop(0, tiles, grad_pass, 0)

    def finish_part(index, carry):
        j, device = index // 4, lax.rem(index, 4)
        owner, side = device // 2, lax.rem(device, 2)
        flip = turned(4 * j + 2 * side + owner)
        at = pl.ds(pl.multiple_of(device * half, half), half)
        low, high = acc[0, j, at], acc[1, j, at]
        scale = jnp.where(
            lax.broadcasted_iota(jnp.int32, (half, 2 * HD), 1) < HD, jnp.float32(scaling), 1.0
        )
        first = jnp.where(flip, high, low) * scale
        second = jnp.where(flip, low, high) * scale
        part[j, owner, side, 0:half] = first.astype(part.dtype)
        part[j, owner, side, half:rows] = second.astype(part.dtype)
        return carry

    lax.fori_loop(0, 4 * depth, finish_part, 0)
    by_core = copies.slots(depth)
    for k in list(range(1, depth)) + [0]:
        copies.send(part.at[far(k), 1 - c], core_in.at[far(k)], by_core + k, core)

    for high in range(2):
        q_turned = (jnp.transpose(dq_acc[high]) * scaling).astype(jnp.bfloat16)
        q_sort[high] = q_turned
    for side in range(2):
        flip = turned(4 * z + 2 * side + c)
        for h in range(GROUP):
            at = (side * GROUP + h) * half
            low, high = q_sort[0, at : at + half], q_sort[1, at : at + half]
            h_q[y, c, side, 0:half, h * HD : (h + 1) * HD] = jnp.where(flip, high, low)
            h_q[y, c, side, half:rows, h * HD : (h + 1) * HD] = jnp.where(flip, low, high)

    def wide(ref):
        return ref[...].astype(jnp.float32)

    by_plane = copies.slots(depth)
    for k in list(range(1, depth)) + [0]:
        j = far(k)
        copies.wait(core_in.at[j], by_core + k, core)
        added = wide(part.at[j, c]) + wide(core_in.at[j])
        if k == 0:
            summed = added
        else:
            sum_out[k] = added.astype(sum_out.dtype)
            copies.send(sum_out.at[k], z_in.at[k], by_plane + k, plane(j))

    def quad_start(ref):
        first = copies.slots(3)
        here = ref.at[y, c]
        copies.send(here, here, first, beside)
        copies.send(here, here, first + 1, core)

        def relay():
            there = ref.at[1 - y, c]
            copies.wait(there, first, beside)
            copies.send(there, there, first + 2, core)

        def finish():
            copies.wait(ref.at[y, 1 - c], first + 1, core)
            copies.wait(ref.at[1 - y, 1 - c], first + 2, core)

        return relay, finish

    q_relay, q_finish = quad_start(h_q)
    w_relay(1)
    q_relay()
    for k in range(1, depth):
        copies.wait(z_in.at[k], by_plane + k, core)
        summed = summed + wide(z_in.at[k])
    h_kv[y, c] = summed.astype(h_kv.dtype)
    kv_relay, kv_finish = quad_start(h_kv)
    for step in range(2, depth - 1):
        w_relay(step)
    kv_relay()
    q_finish()
    kv_finish()

    heads = jnp.concatenate(
        [h_q[g].reshape(4 * rows, WIDE) for g in range(KVH)]
        + [
            h_kv[g, :, :, :, part_of * HD : (part_of + 1) * HD].reshape(4 * rows, HD)
            for part_of in range(2)
            for g in range(KVH)
        ],
        axis=1,
    )
    step_of = jnp.where(2 * z >= depth, depth - 1, 1)
    mine = 2 * y + c
    y_recv = [copies.slots(4 * depth) for _ in range(1)][0]
    for k in range(depth):
        if k == depth - 1:
            w_relay(depth - 1)
        j = lax.rem(z + k * step_of, depth)
        if k > 0:
            w_finish(j, None)
        block = lax.dot_general(
            heads, w_all[j], (((1,), (1,)), ((), ())), preferred_element_type=jnp.float32
        )
        y_out[j] = block.astype(y_out.dtype).reshape(2, 2, rows, shard)
        for device, owner, side in (
            (beside, c, 1 - y),
            (corner, 1 - c, 1 - y),
            (core, 1 - c, y),
        ):
            copies.send(
                y_out.at[j, owner, side], y_in.at[j, mine], y_recv + 4 * j + mine, device
            )
    for k in range(depth):
        j = lax.rem(z + k * step_of, depth)
        for source, device in (
            (2 * y + 1 - c, core),
            (2 * (1 - y) + c, beside),
            (2 * (1 - y) + 1 - c, corner),
        ):
            copies.wait(y_in.at[j, source], y_recv + 4 * j + source, device)
        y_in[j, mine] = y_out[j, c, y]
    for j in range(depth):
        for source in range(4):
            at = (4 * j + source) * shard
            out_ref[:, at : at + shard] = y_in[j, source]
    copies.drain()


def layer_grads(order, mask, queries, out_grad, row_delta, keys, values, weight, count):
    depth = count // 4
    rows = queries.shape[0]
    half = rows // 2
    lanes = 2 * GROUP * half
    shard, qkv = weight.shape
    low, wide = jnp.bfloat16, jnp.float32
    smem = pl.BlockSpec(memory_space=pltpu.SMEM)
    vmem = pl.BlockSpec(memory_space=pltpu.VMEM)
    anywhere = pl.BlockSpec(memory_space=pl.ANY)
    kv_shape = (depth, 2, 2, rows, HD)
    pair = (2, rows, 2 * HD)
    return pl.pallas_call(
        functools.partial(layer_kernel, depth),
        out_shape=jax.ShapeDtypeStruct((rows, count * shard), low),
        in_specs=[smem, smem] + [anywhere] * 6,
        out_specs=vmem,
        scratch_shapes=[
            pltpu.VMEM(kv_shape, low),
            pltpu.VMEM(kv_shape, low),
            pltpu.VMEM((2, rows, WIDE), low),
            pltpu.VMEM((2, rows, WIDE), low),
            pltpu.VMEM((2,) + row_delta.shape, wide),
            pltpu.VMEM((depth, shard, qkv), low),
            pltpu.VMEM((2, depth, 4 * half, HD), low),
            pltpu.VMEM((2, depth, 4 * half, HD), low),
            pltpu.VMEM((2, lanes, HD), low),
            pltpu.VMEM((2, lanes, HD), low),
            pltpu.VMEM((2, 8, lanes), wide),
            pltpu.VMEM((rows, 128), wide),
            pltpu.VMEM((3 * depth, 4 * half, lanes), wide),
            pltpu.VMEM((2, 8, lanes), wide),
            pltpu.VMEM((2, 8, lanes), wide),
            pltpu.VMEM((2, HD, lanes), wide),
            pltpu.VMEM((2, depth, 4 * half, 2 * HD), wide),
            pltpu.VMEM((depth, 2) + pair, low),
            pltpu.VMEM((depth,) + pair, low),
            pltpu.VMEM((depth,) + pair, low),
            pltpu.VMEM((depth,) + pair, low),
            pltpu.VMEM((2, 2, 2, rows, WIDE), low),
            pltpu.VMEM((2, 2, 2, rows, 2 * HD), low),
            pltpu.VMEM((depth, 2, 2, rows, shard), low),
            pltpu.VMEM((depth, 4, rows, shard), low),
            pltpu.SemaphoreType.DMA((6,)),
            pltpu.SemaphoreType.DMA((64 + 64 * depth,)),
            pltpu.SemaphoreType.DMA((64 + 32 * depth,)),
        ],
        compiler_params=pltpu.CompilerParams(
            collective_id=0, has_side_effects=True, vmem_limit_bytes=67043328
        ),
        name="layer_grads",
    )(order, mask, queries, out_grad, row_delta, keys, values, weight)


def swapped(array, axis, apart):
    return lax.ppermute(array, axis, [(i, i ^ 1 << apart) for i in range(lax.axis_size(axis))])


def body(
    queries,
    keys,
    values,
    out_grad,
    row_delta,
    layer_input,
    norm_gain,
    qkv_weight,
    block_order,
    block_mask,
    frame_owner,
    vision_features,
    post_gain,
    projector,
):
    tok_rows = queries.shape[0]
    half_len = tok_rows // 2
    my_index = lax.axis_index("seq")
    my_blocks = lax.dynamic_slice_in_dim(block_order, 2 * my_index, 2, 0)
    count = lax.axis_size("seq")
    norm_grad = layer_grads(
        block_order, block_mask, queries, out_grad, row_delta, keys, values, qkv_weight, count
    )
    inputs = layer_input.astype(jnp.float32)
    inverse = lax.rsqrt(jnp.mean(inputs * inputs, axis=1, keepdims=True) + EPSILON)
    scaled = norm_grad.astype(jnp.float32) * norm_gain
    token_grad = (
        inverse * scaled - inputs * inverse**3 * jnp.mean(scaled * inputs, axis=1, keepdims=True)
    ).astype(jnp.bfloat16)
    frame_table = jnp.arange(frame_owner.shape[0], dtype=jnp.int32)
    my_frame = jnp.sum(jnp.where(frame_owner == my_index, frame_table, 0))
    keep_first = my_blocks[0] // 2 == my_frame
    kept_block = jnp.where(keep_first, my_blocks[0], my_blocks[1])
    leading = kept_block % 2 == 0
    halves = token_grad.reshape(2, half_len, token_grad.shape[1])
    kept = jnp.where(keep_first, halves[0], halves[1])
    sending = jnp.where(keep_first, halves[1], halves[0])
    received = swapped(sending, "seq", 0)
    frame_rows = jnp.where(
        leading,
        jnp.concatenate([kept, received], axis=0),
        jnp.concatenate([received, kept], axis=0),
    )
    post_grad = jnp.dot(frame_rows, projector.T, preferred_element_type=jnp.float32)
    features = vision_features[0].astype(jnp.float32)
    centered = features - jnp.mean(features, axis=1, keepdims=True)
    deviation = lax.rsqrt(jnp.mean(centered * centered, axis=1, keepdims=True) + EPSILON)
    normed = centered * deviation
    weighted = post_grad * post_gain
    encoder_grad = (
        deviation
        * (
            weighted
            - jnp.mean(weighted, axis=1, keepdims=True)
            - normed * jnp.mean(weighted * normed, axis=1, keepdims=True)
        )
    ).astype(jnp.bfloat16)
    return (token_grad, encoder_grad[None])


def solution(mesh):
    placed = (
        P(("batch", "seq"), None),
        P(("batch", "seq"), None),
        P(("batch", "seq"), None),
        P(("batch", "seq"), None),
        P(("batch", "seq"), None),
        P(("batch", "seq"), None),
        P(),
        P("seq", None),
        P("batch"),
        P("batch", None),
        P("batch"),
        P(("batch", "seq"), None, None),
        P(),
        P(),
    )
    return jax.shard_map(
        body,
        mesh=mesh,
        in_specs=placed,
        out_specs=(P(("batch", "seq"), None), P(("batch", "seq"), None, None)),
        check_vma=False,
    )
```

time: 148 us -> 104 us (0.70)
  Pallas kernels: 118 us -> 83.7 us
  matrix products: 17.4 us -> 6.14 us
  other arithmetic: 3.68 us -> 5.43 us
    pallas_call x3 -> x1, Pallas kernels: 118 us -> 83.7 us  [layer_grads(): pl.pallas_call(functools.partial(layer_kernel, depth), out_shape=jax.Shap...]
    dot_general x1 -> x0, matrix products: 11.2 us -> none  [body(): jnp.dot(head_grads, weight.T, preferred_element_type=jnp.float32)]
    reduce_sum x0 -> x1, other arithmetic: none -> 2.1 us  [body(): jnp.mean(inputs * inputs, axis=1, keepdims=True) + EPSILON]
where the time goes in v1:
time: 104 us
  Pallas kernels  83.7 us (80%)
  matrix products  6.14 us (6%)
  other arithmetic  5.43 us (5%)
  between operations  5.42 us (5%)
  local copies, waits for them, and re-layouts  2.81 us (3%)
    pallas_call x1, Pallas kernels, layer_grads(): pl.pallas_call(functools.partial(layer_kernel, depth), out_shape=jax.Shap...  83.7 us
    dot_general x1, matrix products, body(): jnp.dot(frame_rows, projector.T, preferred_element_type=jnp.float32)  6.14 us
    reduce_sum x1, other arithmetic, body(): jnp.mean(inputs * inputs, axis=1, keepdims=True) + EPSILON  2.1 us
  transfers between devices with their start and end apart: 1, of which 0 were waited for; matrix products, arithmetic and copies ran while one was open for 0% of the time, Pallas kernels for 0%

profile of v1, /device:TPU:0, one launch (start us, length us, event | category | flops | bytes accessed | tf_op | source)
XLA Modules:
  0.0 104.1 jit_solution(15491001542865427002)
XLA Ops:
  0.6 0.7 dynamic_slice.3
  1.4 0.6 fusion.25
  4.7 1.3 %fusion.22 = s32[]{:T(128)} fusion(s32[16]{0:T(128)} %param.24, s32[]{:T(128)S(6)} %axis_index.15), kind=kLoop, calls=%fused_computation.34 | loop fusion | flops 47 | bytes 72 | tf_op jit(solution)/shard_map/reduce_sum | solution.py:617
  6.0 1.4 %copy.16.delta_hbm = f32[128,14]{1,0:T(8,128)} copy(f32[128,14]{0,1:T(8,128)} %param.18) | data formatting | bytes 14336 | tf_op args[4]
  8.1 83.7 %layer_grads.1 = bf16[128,3584]{1,0:T(8,128)(2,1)} custom-call(s32[32]{0:T(128)} %order_ref.1, s32[32,32]{1,0:T(8,128)} %mask_ref.1, bf16[128,1792]{1,0:T(8,128)(2,1)} %queries_ref.1, bf16[128,1792]{1,0:T(8,128)(2,1)} %grads_ref.1, f32[128,14]{1,0:T(8,128)} %copy.16.delta_hbm, bf16[128,256]{1,0:T(8,128)(2,1)} %keys_ref.1, bf16[128,256]{1,0:T(8,128)(2,1)} %values_ref.1, ...), custom_call_target="tpu_custom_call" | custom-call | tf_op jit(solution)/shard_map/layer_grads/pallas_call | solution.py:540
  91.8 0.0 copy-start
  91.8 0.0 copy-start.1
  91.8 0.0 copy-start.4
  91.8 2.1 %fusion = (f32[128]{0:T(128)S(1)}, f32[128]{0:T(128)S(1)}) fusion(bf16[128,3584]{1,0:T(8,128)(2,1)} %param.19, f32[3584]{0:T(1024)} %param.20, bf16[128,3584]{1,0:T(8,128)(2,1)} %layer_grads.1), kind=kLoop, calls=%fused_computation.4 | loop fusion | flops 3211008 | bytes 1850368 | tf_op jit(solution)/shard_map/reduce_sum | solution.py:611
  93.9 0.0 copy-done
  93.9 0.0 copy-done.1
  93.9 0.0 copy-done.4
  93.9 0.0 copy-start.3
  94.0 0.6 fusion.3
  94.6 0.0 copy-start.2
  94.6 0.0 copy-start.5
  94.6 0.1 broadcast_select_fusion.1
  94.7 0.6 collective-permute-start
  95.3 0.0 copy-done.3
  95.3 0.1 convert_reduce_fusion
  96.7 0.2 fusion.20
  96.9 0.0 collective-permute-done
  96.9 0.0 copy-done.5
  97.0 6.1 %fusion.24 = (f32[128]{0:T(128)S(1)}, f32[128]{0:T(128)S(1)}, f32[128,1152]{1,0:T(8,128)S(1)}) fusion(f32[128]{0:T(128)S(1)} %add_rsqrt_fusion, f32[128]{0:T(128)S(1)} %broadcast_multiply_fusion.2, bf16[1,128,1152]{2,1,0:T(8,128)(2,1)S(1)} %copy-done.3, f32[1152]{0:T(1024)S(1)} %copy-done.5, bf16[1152,3584]{1,0:T(8,128)(2,1)} %param.27, ...), kind=kOutput, calls=%fused_computation.42 | convolution fusion | flops 1062125312 | bytes 10066433 | tf_op jit(solution)/shard_map/dot_general | solution.py:630
  103.1 0.0 copy-done.2
  103.1 1.0 fusion.21
  (5 shorter events, 0.0 us)
Async XLA Ops:
  91.8 2.1 %copy-start = (bf16[128,3584]{1,0:T(8,128)(2,1)S(1)}, bf16[128,3584]{1,0:T(8,128)(2,1)}, u32[]{:S(2)}) copy-start(bf16[128,3584]{1,0:T(8,128)(2,1)} %layer_grads.1) | copy-start | bytes 2752516
  91.8 2.1 %copy-start.1 = (bf16[128,3584]{1,0:T(8,128)(2,1)S(1)}, bf16[128,3584]{1,0:T(8,128)(2,1)}, u32[]{:S(2)}) copy-start(bf16[128,3584]{1,0:T(8,128)(2,1)} %param.19) | copy-start | bytes 2752516
  91.8 2.1 %copy-start.4 = (f32[3584]{0:T(1024)S(1)}, f32[3584]{0:T(1024)}, u32[]{:S(2)}) copy-start(f32[3584]{0:T(1024)} %param.20) | copy-start | bytes 43012
  93.9 1.3 %copy-start.3 = (bf16[1,128,1152]{2,1,0:T(8,128)(2,1)S(1)}, bf16[1,128,1152]{2,1,0:T(8,128)(2,1)}, u32[]{:S(2)}) copy-start(bf16[1,128,1152]{2,1,0:T(8,128)(2,1)} %param.25) | copy-start | bytes 884740
  94.6 8.5 %copy-start.2 = (bf16[128,3584]{1,0:T(8,128)(2,1)}, bf16[128,3584]{1,0:T(8,128)(2,1)S(1)}, u32[]{:S(2)}) copy-start(bf16[128,3584]{1,0:T(8,128)(2,1)S(1)} %fusion.3) | copy-start | bytes 2752516
  94.6 2.4 %copy-start.5 = (f32[1152]{0:T(1024)S(1)}, f32[1152]{0:T(1024)}, u32[]{:S(2)}) copy-start(f32[1152]{0:T(1024)} %param.26) | copy-start | bytes 13828
  94.7 2.3 %collective-permute-start = (bf16[64,3584]{1,0:T(8,128)(2,1)S(1)}, bf16[64,3584]{1,0:T(8,128)(2,1)S(1)}, u32[]{:S(2)}, u32[]{:S(2)}) collective-permute-start(bf16[64,3584]{1,0:T(8,128)(2,1)S(1)} %get-tuple-element.7), channel_id=1, source_target_pairs={{0,2},{2,0},{4,6},{6,4},{8,10},{10,8},{12,14},{14,12},{16,18},{18,... | collective-permute-start | bytes 1376264 | tf_op jit(solution)/shard_map/ppermute | solution.py:583

commit v2 on v1

--- a/solution.py
+++ b/solution.py
@@ -15,7 +15,7 @@
 LOG2E = 1.4426950408889634
 EPSILON = 1e-06
 NEGATIVE = -1e30
-PIECES = 3
+PIECES = 4
 MESH = pl.DeviceIdType.MESH
 
 
@@ -73,6 +73,7 @@
 
 def layer_kernel(
     depth,
+    counts,
     order_ref,
     mask_ref,
     queries_ref,
@@ -82,6 +83,7 @@
     values_ref,
     weight_ref,
     out_ref,
+    kv_swap,
     k_all,
     v_all,
     q_in,
@@ -93,7 +95,6 @@
     q_sort,
     g_sort,
     d_sort,
-    d_pad,
     scores,
     top,
     total,
@@ -145,6 +146,10 @@
         copy.start()
         return copy
 
+    load_swap = [
+        load(head_at(ref, 1 - y, HD), kv_swap.at[i], 6 + i)
+        for i, ref in enumerate((keys_ref, values_ref))
+    ]
     load_k = load(head_at(keys_ref, y, HD), k_all.at[z, c, y], 0)
     load_v = load(head_at(values_ref, y, HD), v_all.at[z, c, y], 1)
     load_w = load(weight_ref, w_all.at[z], 2)
@@ -161,8 +166,9 @@
     copies = Copies(send_sem, recv_sem)
 
     over_y = copies.slots(5)
-    copies.send(head_at(keys_ref, 1 - y, HD), k_all.at[z, c, y], over_y, beside)
-    copies.send(head_at(values_ref, 1 - y, HD), v_all.at[z, c, y], over_y + 1, beside)
+    for i, ref in enumerate((k_all, v_all)):
+        load_swap[i].wait()
+        copies.send(kv_swap.at[i], ref.at[z, c, y], over_y + i, beside)
     copies.send(head_at(queries_ref, 1 - y, WIDE), q_in.at[y], over_y + 2, beside)
     copies.send(head_at(grads_ref, 1 - y, WIDE), g_in.at[y], over_y + 3, beside)
     copies.send(delta_hbm, d_in.at[y], over_y + 4, beside)
@@ -227,34 +233,49 @@
     w_recv = [copies.slots(depth) for _ in range(count + 1)]
     w_cross = [copies.slots(depth) for _ in range(count)]
 
-    def w_send(j, upward, downward):
-        for i in range(count + (between > 0)):
+    parts = list(range(count + (between > 0)))
+
+    def w_send(j, upward, downward, some):
+        for i in some:
             ref = w_at(j, x, *pieces[i]) if i < count else w_middle(j)
             if upward is not None:
                 copies.send(ref, ref, w_recv[i] + j, up, upward)
             if downward is not None:
                 copies.send(ref, ref, w_recv[i] + j, down, downward)
 
-    def w_relay(step):
+    def w_line(step, i):
         for j, present, upward in (
             (z - step, z - step >= 0, True),
             (z + step, z + step < depth, False),
         ):
             at = jnp.clip(j, 0, depth - 1)
+            ref = w_at(at, x, *pieces[i]) if i < count else w_middle(at)
+            yield at, present, upward, ref
+
+    def w_take(step, i):
+        for at, present, upward, ref in w_line(step, i):
+            copies.wait(ref, w_recv[i] + at, core, present)
+            if i < count:
+                copies.send(ref, ref, w_cross[i] + at, across, present)
+
+    def w_pass(step, i):
+        if step == depth - 1:
+            return
+        for at, present, upward, ref in w_line(step, i):
             go = jnp.logical_and(present, has_up if upward else has_down)
-            for i in range(count + (between > 0)):
-                ref = w_at(at, x, *pieces[i]) if i < count else w_middle(at)
-                copies.wait(ref, w_recv[i] + at, core, present)
-                copies.send(ref, ref, w_recv[i] + at, up if upward else down, go)
-                if i < count:
-                    copies.send(ref, ref, w_cross[i] + at, across, present)
+            copies.send(ref, ref, w_recv[i] + at, up if upward else down, go)
+
+    def w_relay(step, some):
+        for i in some:
+            w_take(step, i)
+            w_pass(step, i)
 
     def w_finish(j, other):
         for i in range(count):
             copies.wait(w_at(j, 1 - x, *pieces[i]), w_cross[i] + j, across, other)
 
     load_w.wait()
-    w_send(z, has_up, has_down)
+    w_send(z, has_up, has_down, parts)
 
     def turned(device):
         return order_ref[2 * device] > order_ref[2 * device + 1]
@@ -366,12 +387,9 @@
     copies.wait(d_in.at[1 - y], over_y + 4, beside)
     for side in range(2):
         arrange(g_in, g_sort, side)
-        d_pad[...] = jnp.zeros_like(d_pad)
-        d_pad[:, 0 : d_in.shape[2]] = d_in[side]
-        flipped = jnp.transpose(d_pad[...])
         flip = turned(4 * z + 2 * side + c)
         for h in range(GROUP):
-            line = jnp.where(y == 1, flipped[GROUP + h : GROUP + h + 1], flipped[h : h + 1])
+            line = jnp.where(y == 1, d_in[side, GROUP + h : GROUP + h + 1], d_in[side, h : h + 1])
             first, second = line[:, 0:half], line[:, half:rows]
             at = (side * GROUP + h) * half
             d_sort[0, :, at : at + half] = spread_rows(jnp.where(flip, second, first))
@@ -401,27 +419,47 @@
         )
         return carry
 
-    lax.fori_loop(0, tiles, grad_pass, 0)
-
-    def finish_part(index, carry):
-        j, device = index // 4, lax.rem(index, 4)
-        owner, side = device // 2, lax.rem(device, 2)
-        flip = turned(4 * j + 2 * side + owner)
-        at = pl.ds(pl.multiple_of(device * half, half), half)
-        low, high = acc[0, j, at], acc[1, j, at]
-        scale = jnp.where(
-            lax.broadcasted_iota(jnp.int32, (half, 2 * HD), 1) < HD, jnp.float32(scaling), 1.0
-        )
-        first = jnp.where(flip, high, low) * scale
-        second = jnp.where(flip, low, high) * scale
-        part[j, owner, side, 0:half] = first.astype(part.dtype)
-        part[j, owner, side, half:rows] = second.astype(part.dtype)
-        return carry
-
-    lax.fori_loop(0, 4 * depth, finish_part, 0)
-    by_core = copies.slots(depth)
-    for k in list(range(1, depth)) + [0]:
-        copies.send(part.at[far(k), 1 - c], core_in.at[far(k)], by_core + k, core)
+    scale = jnp.where(
+        lax.broadcasted_iota(jnp.int32, (half, 2 * HD), 1) < HD, jnp.float32(scaling), 1.0
+    )
+
+    def finish_part(j):
+        for device in range(4):
+            owner, side = device // 2, device % 2
+            flip = turned(4 * j + 2 * side + owner)
+            at = slice(device * half, (device + 1) * half)
+            low, high = acc[0, j, at], acc[1, j, at]
+            first = jnp.where(flip, high, low) * scale
+            second = jnp.where(flip, low, high) * scale
+            part[j, owner, side, 0:half] = first.astype(part.dtype)
+            part[j, owner, side, half:rows] = second.astype(part.dtype)
+
+    def wide(ref):
+        return ref[...].astype(jnp.float32)
+
+    by_core, by_plane = copies.slots(depth), copies.slots(depth)
+
+    def add_cores(k):
+        j = far(k)
+        copies.wait(core_in.at[j], by_core + k, core)
+        added = wide(part.at[j, c]) + wide(core_in.at[j])
+        if k > 0:
+            sum_out[k] = added.astype(sum_out.dtype)
+            copies.send(sum_out.at[k], z_in.at[k], by_plane + k, plane(j))
+        return added
+
+    order = list(range(1, depth)) + [0]
+    taken = 0
+    for index, k in enumerate(order):
+        j = far(k)
+        lax.fori_loop(0, 3, lambda kind, carry: grad_pass(kind * depth + j, carry), 0)
+        finish_part(j)
+        copies.send(part.at[j, 1 - c], core_in.at[j], by_core + k, core)
+        if index > 0:
+            add_cores(order[index - 1])
+        if index < len(parts) - 1:
+            w_take(1, parts[index])
+            taken = index + 1
 
     for high in range(2):
         q_turned = (jnp.transpose(dq_acc[high]) * scaling).astype(jnp.bfloat16)
@@ -434,20 +472,6 @@
             h_q[y, c, side, 0:half, h * HD : (h + 1) * HD] = jnp.where(flip, high, low)
             h_q[y, c, side, half:rows, h * HD : (h + 1) * HD] = jnp.where(flip, low, high)
 
-    def wide(ref):
-        return ref[...].astype(jnp.float32)
-
-    by_plane = copies.slots(depth)
-    for k in list(range(1, depth)) + [0]:
-        j = far(k)
-        copies.wait(core_in.at[j], by_core + k, core)
-        added = wide(part.at[j, c]) + wide(core_in.at[j])
-        if k == 0:
-            summed = added
-        else:
-            sum_out[k] = added.astype(sum_out.dtype)
-            copies.send(sum_out.at[k], z_in.at[k], by_plane + k, plane(j))
-
     def quad_start(ref):
         first = copies.slots(3)
         here = ref.at[y, c]
@@ -466,15 +490,31 @@
         return relay, finish
 
     q_relay, q_finish = quad_start(h_q)
-    w_relay(1)
-    q_relay()
+    summed = add_cores(0)
+    for i in parts[taken:]:
+        w_take(1, i)
+    for i in parts:
+        w_pass(1, i)
+
     for k in range(1, depth):
         copies.wait(z_in.at[k], by_plane + k, core)
         summed = summed + wide(z_in.at[k])
     h_kv[y, c] = summed.astype(h_kv.dtype)
     kv_relay, kv_finish = quad_start(h_kv)
-    for step in range(2, depth - 1):
-        w_relay(step)
+    near = list(range(2, depth - 1))
+    for step in near[:-1]:
+        w_relay(step, parts)
+    cuts = [len(parts) * i // 4 for i in range(5)]
+    groups = [parts[a:b] for a, b in zip(cuts, cuts[1:])]
+
+    def w_some(index):
+        if near:
+            w_relay(near[-1], groups[index])
+
+    w_some(0)
+    q_relay()
+    w_some(1)
+    w_some(2)
     kv_relay()
     q_finish()
     kv_finish()
@@ -490,10 +530,9 @@
     )
     step_of = jnp.where(2 * z >= depth, depth - 1, 1)
     mine = 2 * y + c
-    y_recv = [copies.slots(4 * depth) for _ in range(1)][0]
-    for k in range(depth):
-        if k == depth - 1:
-            w_relay(depth - 1)
+    y_recv = copies.slots(4 * depth)
+
+    def multiply(k):
         j = lax.rem(z + k * step_of, depth)
         if k > 0:
             w_finish(j, None)
@@ -509,7 +548,8 @@
             copies.send(
                 y_out.at[j, owner, side], y_in.at[j, mine], y_recv + 4 * j + mine, device
             )
-    for k in range(depth):
+
+    def collect(k):
         j = lax.rem(z + k * step_of, depth)
         for source, device in (
             (2 * y + 1 - c, core),
@@ -518,14 +558,32 @@
         ):
             copies.wait(y_in.at[j, source], y_recv + 4 * j + source, device)
         y_in[j, mine] = y_out[j, c, y]
+
+    for k in range(depth - 1):
+        if k == depth - 2:
+            w_relay(depth - 1, groups[0])
+            w_relay(depth - 1, groups[1])
+        multiply(k)
+        if k == 0:
+            w_some(3)
+    w_relay(depth - 1, groups[2])
+    collect(0)
+    w_relay(depth - 1, groups[3])
+    for k in range(1, depth - 1):
+        collect(k)
+    multiply(depth - 1)
+    collect(depth - 1)
+
     for j in range(depth):
         for source in range(4):
             at = (4 * j + source) * shard
             out_ref[:, at : at + shard] = y_in[j, source]
     copies.drain()
-
-
-def layer_grads(order, mask, queries, out_grad, row_delta, keys, values, weight, count):
+    counts.append((copies.sends, copies.recvs))
+
+
+def layer_grads(arguments, count):
+    order, mask, queries, out_grad, row_delta, keys, values, weight = arguments
     depth = count // 4
     rows = queries.shape[0]
     half = rows // 2
@@ -537,12 +595,14 @@
     anywhere = pl.BlockSpec(memory_space=pl.ANY)
     kv_shape = (depth, 2, 2, rows, HD)
     pair = (2, rows, 2 * HD)
-    return pl.pallas_call(
-        functools.partial(layer_kernel, depth),
+    def build(counts, sends, recvs):
+        return pl.pallas_call(
+        functools.partial(layer_kernel, depth, counts),
         out_shape=jax.ShapeDtypeStruct((rows, count * shard), low),
         in_specs=[smem, smem] + [anywhere] * 6,
         out_specs=vmem,
         scratch_shapes=[
+            pltpu.VMEM((2, rows, HD), low),
             pltpu.VMEM(kv_shape, low),
             pltpu.VMEM(kv_shape, low),
             pltpu.VMEM((2, rows, WIDE), low),
@@ -554,7 +614,6 @@
             pltpu.VMEM((2, lanes, HD), low),
             pltpu.VMEM((2, lanes, HD), low),
             pltpu.VMEM((2, 8, lanes), wide),
-            pltpu.VMEM((rows, 128), wide),
             pltpu.VMEM((3 * depth, 4 * half, lanes), wide),
             pltpu.VMEM((2, 8, lanes), wide),
             pltpu.VMEM((2, 8, lanes), wide),
@@ -568,15 +627,19 @@
             pltpu.VMEM((2, 2, 2, rows, 2 * HD), low),
             pltpu.VMEM((depth, 2, 2, rows, shard), low),
             pltpu.VMEM((depth, 4, rows, shard), low),
-            pltpu.SemaphoreType.DMA((6,)),
-            pltpu.SemaphoreType.DMA((64 + 64 * depth,)),
-            pltpu.SemaphoreType.DMA((64 + 32 * depth,)),
+            pltpu.SemaphoreType.DMA((13,)),
+            pltpu.SemaphoreType.DMA((sends,)),
+            pltpu.SemaphoreType.DMA((recvs,)),
         ],
         compiler_params=pltpu.CompilerParams(
             collective_id=0, has_side_effects=True, vmem_limit_bytes=67043328
         ),
         name="layer_grads",
-    )(order, mask, queries, out_grad, row_delta, keys, values, weight)
+    )
+
+    counts = []
+    jax.eval_shape(build(counts, 4096, 4096), *arguments)
+    return build([], *counts[0])(*arguments)
 
 
 def swapped(array, axis, apart):
@@ -599,14 +662,21 @@
     post_gain,
     projector,
 ):
+    arguments = (
+        block_order,
+        block_mask,
+        queries,
+        out_grad,
+        row_delta.T,
+        keys,
+        values,
+        qkv_weight,
+    )
     tok_rows = queries.shape[0]
     half_len = tok_rows // 2
     my_index = lax.axis_index("seq")
     my_blocks = lax.dynamic_slice_in_dim(block_order, 2 * my_index, 2, 0)
-    count = lax.axis_size("seq")
-    norm_grad = layer_grads(
-        block_order, block_mask, queries, out_grad, row_delta, keys, values, qkv_weight, count
-    )
+    norm_grad = layer_grads(arguments, lax.axis_size("seq"))
     inputs = layer_input.astype(jnp.float32)
     inverse = lax.rsqrt(jnp.mean(inputs * inputs, axis=1, keepdims=True) + EPSILON)
     scaled = norm_grad.astype(jnp.float32) * norm_gain

time: 104 us -> 94.4 us (0.908)
  Pallas kernels: 83.7 us -> 75.6 us
  local copies, waits for them, and re-layouts: 2.81 us -> 1.35 us
    pallas_call x1, Pallas kernels: 83.7 us -> 75.6 us  [layer_grads(): return build([], *counts[0])(*arguments)]
    unnamed x13 -> x12, local copies, waits for them, and re-layouts: 1.46 us -> 0.04 us
where the time goes in v2:
time: 94.4 us; the launch traced here: 94.1 us
  Pallas kernels  75.6 us (80%)
  matrix products  6.14 us (7%)
  other arithmetic  5.43 us (6%)
  between operations  5.13 us (5%)
  local copies, waits for them, and re-layouts  1.35 us (1%)
    pallas_call x1, Pallas kernels, layer_grads(): return build([], *counts[0])(*arguments)  75.6 us
    dot_general x1, matrix products, body(): jnp.dot(frame_rows, projector.T, preferred_element_type=jnp.float32)  6.14 us
    reduce_sum x1, other arithmetic, body(): jnp.mean(inputs * inputs, axis=1, keepdims=True) + EPSILON  2.1 us
  transfers between devices with their start and end apart: 1, of which 0 were waited for; matrix products, arithmetic and copies ran while one was open for 0% of the time, Pallas kernels for 0%

profile of v2, /device:TPU:0, one launch (start us, length us, event | category | flops | bytes accessed | tf_op | source)
XLA Modules:
  0.0 94.1 jit_solution(10482357191053370311)
XLA Ops:
  0.6 0.7 dynamic_slice.3
  1.4 0.6 fusion.25
  4.4 1.3 %fusion.22 = s32[]{:T(128)} fusion(s32[16]{0:T(128)} %param.24, s32[]{:T(128)S(6)} %axis_index.15), kind=kLoop, calls=%fused_computation.34 | loop fusion | flops 47 | bytes 72 | tf_op jit(solution)/shard_map/reduce_sum | solution.py:687
  6.3 75.6 %layer_grads.1 = bf16[128,3584]{1,0:T(8,128)(2,1)} custom-call(s32[32]{0:T(128)} %order_ref.1, s32[32,32]{1,0:T(8,128)} %mask_ref.1, bf16[128,1792]{1,0:T(8,128)(2,1)} %queries_ref.1, bf16[128,1792]{1,0:T(8,128)(2,1)} %grads_ref.1, f32[14,128]{1,0:T(8,128)} %bitcast.30, bf16[128,256]{1,0:T(8,128)(2,1)} %keys_ref.1, bf16[128,256]{1,0:T(8,128)(2,1)} %values_ref.1, ...), custom_call_target="tpu_custom_call" | custom-call | tf_op jit(solution)/shard_map/layer_grads/pallas_call | solution.py:642
  81.9 0.0 copy-start
  81.9 0.0 copy-start.1
  81.9 0.0 copy-start.4
  81.9 2.1 %fusion = (f32[128]{0:T(128)S(1)}, f32[128]{0:T(128)S(1)}) fusion(bf16[128,3584]{1,0:T(8,128)(2,1)} %param.19, f32[3584]{0:T(1024)} %param.20, bf16[128,3584]{1,0:T(8,128)(2,1)} %layer_grads.1), kind=kLoop, calls=%fused_computation.4 | loop fusion | flops 3211008 | bytes 1850368 | tf_op jit(solution)/shard_map/reduce_sum | solution.py:681
  84.1 0.0 copy-done
  84.1 0.0 copy-done.1
  84.1 0.0 copy-done.4
  84.1 0.0 copy-start.3
  84.1 0.6 fusion.3
  84.7 0.0 copy-start.2
  84.8 0.0 copy-start.5
  84.8 0.1 broadcast_select_fusion.1
  84.8 0.5 collective-permute-start
  85.3 0.0 copy-done.3
  85.3 0.1 convert_reduce_fusion
  86.7 0.2 fusion.20
  86.9 0.0 collective-permute-done
  87.0 0.0 copy-done.5
  87.0 6.1 %fusion.24 = (f32[128]{0:T(128)S(1)}, f32[128]{0:T(128)S(1)}, f32[128,1152]{1,0:T(8,128)S(1)}) fusion(f32[128]{0:T(128)S(1)} %add_rsqrt_fusion, f32[128]{0:T(128)S(1)} %broadcast_multiply_fusion.2, bf16[1,128,1152]{2,1,0:T(8,128)(2,1)S(1)} %copy-done.3, f32[1152]{0:T(1024)S(1)} %copy-done.5, bf16[1152,3584]{1,0:T(8,128)(2,1)} %param.27, ...), kind=kOutput, calls=%fused_computation.42 | convolution fusion | flops 1062125312 | bytes 10066433 | tf_op jit(solution)/shard_map/dot_general | solution.py:700
  93.1 0.0 copy-done.2
  93.1 1.0 %fusion.21 = bf16[1,128,1152]{2,1,0:T(8,128)(2,1)} fusion(bf16[1,128,1152]{2,1,0:T(8,128)(2,1)S(1)} %copy-done.3, f32[128,1152]{1,0:T(8,128)S(1)} %get-tuple-element.12, f32[128]{0:T(128)S(1)} %broadcast_multiply_fusion, f32[128]{0:T(128)S(1)} %broadcast_multiply_fusion.1, f32[128]{0:T(128)S(1)} %add_rsqrt_fusion, f32[128]{0:T(128)S(1)} %broadcast_multiply_fusion.2), kind=kLoop, calls=%fused_computation.31 | loop fusion | flops 1179648 | bytes 1181696 | tf_op jit(solution)/shard_map/broadcast_in_dim | solution.py:714
  (5 shorter events, 0.0 us)
Async XLA Ops:
  81.9 2.1 %copy-start = (bf16[128,3584]{1,0:T(8,128)(2,1)S(1)}, bf16[128,3584]{1,0:T(8,128)(2,1)}, u32[]{:S(2)}) copy-start(bf16[128,3584]{1,0:T(8,128)(2,1)} %layer_grads.1) | copy-start | bytes 2752516
  81.9 2.1 %copy-start.1 = (bf16[128,3584]{1,0:T(8,128)(2,1)S(1)}, bf16[128,3584]{1,0:T(8,128)(2,1)}, u32[]{:S(2)}) copy-start(bf16[128,3584]{1,0:T(8,128)(2,1)} %param.19) | copy-start | bytes 2752516
  81.9 2.1 %copy-start.4 = (f32[3584]{0:T(1024)S(1)}, f32[3584]{0:T(1024)}, u32[]{:S(2)}) copy-start(f32[3584]{0:T(1024)} %param.20) | copy-start | bytes 43012
  84.1 1.2 %copy-start.3 = (bf16[1,128,1152]{2,1,0:T(8,128)(2,1)S(1)}, bf16[1,128,1152]{2,1,0:T(8,128)(2,1)}, u32[]{:S(2)}) copy-start(bf16[1,128,1152]{2,1,0:T(8,128)(2,1)} %param.25) | copy-start | bytes 884740
  84.7 8.4 %copy-start.2 = (bf16[128,3584]{1,0:T(8,128)(2,1)}, bf16[128,3584]{1,0:T(8,128)(2,1)S(1)}, u32[]{:S(2)}) copy-start(bf16[128,3584]{1,0:T(8,128)(2,1)S(1)} %fusion.3) | copy-start | bytes 2752516
  84.8 2.2 %copy-start.5 = (f32[1152]{0:T(1024)S(1)}, f32[1152]{0:T(1024)}, u32[]{:S(2)}) copy-start(f32[1152]{0:T(1024)} %param.26) | copy-start | bytes 13828
  84.8 2.1 %collective-permute-start = (bf16[64,3584]{1,0:T(8,128)(2,1)S(1)}, bf16[64,3584]{1,0:T(8,128)(2,1)S(1)}, u32[]{:S(2)}, u32[]{:S(2)}) collective-permute-start(bf16[64,3584]{1,0:T(8,128)(2,1)S(1)} %get-tuple-element.7), channel_id=1, source_target_pairs={{0,2},{2,0},{4,6},{6,4},{8,10},{10,8},{12,14},{14,12},{16,18},{18,... | collective-permute-start | bytes 1376264 | tf_op jit(solution)/shard_map/ppermute | solution.py:646

commit v3 on v2

--- a/solution.py
+++ b/solution.py
@@ -82,7 +82,16 @@
     keys_ref,
     values_ref,
     weight_ref,
-    out_ref,
+    input_ref,
+    gain_ref,
+    owner_ref,
+    features_ref,
+    post_ref,
+    projector_ref,
+    token_ref,
+    encoder_ref,
+    gain_in,
+    post_in,
     kv_swap,
     k_all,
     v_all,
@@ -108,6 +117,19 @@
     h_kv,
     y_out,
     y_in,
+    x_in,
+    x_cut,
+    gain_cut,
+    inverse,
+    norm_cut,
+    token,
+    sending,
+    received,
+    features,
+    normed,
+    deviation,
+    project,
+    encoder,
     load_sem,
     send_sem,
     recv_sem,
@@ -156,6 +178,9 @@
     load_q = load(head_at(queries_ref, y, WIDE), q_in.at[y], 3)
     load_g = load(head_at(grads_ref, y, WIDE), g_in.at[y], 4)
     load_d = load(delta_hbm, d_in.at[y], 5)
+    load_x = load(input_ref, x_in, 8)
+    load_f = load(features_ref.at[0], features, 9)
+    load_n = [load(gain_ref, gain_in, 13), load(post_ref, post_in, 14)]
 
     barrier = pltpu.get_barrier_semaphore()
     peers = [beside, core, corner, across] + [plane(far(k)) for k in range(1, depth)]
@@ -361,6 +386,7 @@
         top[query_high] = best
         return carry
 
+    load_p = load(projector_ref, project, 12)
     lax.fori_loop(0, tiles, score_pass, 0)
     v_relay()
     for high in range(2):
@@ -496,6 +522,27 @@
     for i in parts:
         w_pass(1, i)
 
+    width = 4 * shard
+    model = depth * width
+    for copy in [load_x, load_f] + load_n:
+        copy.wait()
+    gain = gain_in[...].reshape(1, model)
+    squares = jnp.zeros((rows, 1), jnp.float32)
+    for j in range(depth):
+        block = x_in[:, j * width : (j + 1) * width]
+        x_cut[j] = block
+        block = block.astype(jnp.float32)
+        squares += jnp.sum(block * block, axis=1, keepdims=True)
+        gain_cut[j] = jnp.broadcast_to(
+            gain[:, j * width : (j + 1) * width], (8, width)
+        )
+    inverse[...] = jnp.broadcast_to(lax.rsqrt(squares / model + EPSILON), inverse.shape)
+    seen = features[...].astype(jnp.float32)
+    centered = seen - jnp.mean(seen, axis=1, keepdims=True)
+    spread_of = lax.rsqrt(jnp.mean(centered * centered, axis=1, keepdims=True) + EPSILON)
+    normed[...] = centered * spread_of
+    deviation[...] = jnp.broadcast_to(spread_of, deviation.shape)
+
     for k in range(1, depth):
         copies.wait(z_in.at[k], by_plane + k, core)
         summed = summed + wide(z_in.at[k])
@@ -549,7 +596,7 @@
                 y_out.at[j, owner, side], y_in.at[j, mine], y_recv + 4 * j + mine, device
             )
 
-    def collect(k):
+    def collect(k, dots):
         j = lax.rem(z + k * step_of, depth)
         for source, device in (
             (2 * y + 1 - c, core),
@@ -558,7 +605,12 @@
         ):
             copies.wait(y_in.at[j, source], y_recv + 4 * j + source, device)
         y_in[j, mine] = y_out[j, c, y]
-
+        block = jnp.concatenate([wide(y_in.at[j, source]) for source in range(4)], axis=1)
+        block = block * gain_cut[j][0:1]
+        norm_cut[j] = block
+        return dots + jnp.sum(block * x_cut[j].astype(jnp.float32), axis=1, keepdims=True)
+
+    dots = jnp.zeros((rows, 1), jnp.float32)
     for k in range(depth - 1):
         if k == depth - 2:
             w_relay(depth - 1, groups[0])
@@ -567,23 +619,73 @@
         if k == 0:
             w_some(3)
     w_relay(depth - 1, groups[2])
-    collect(0)
+    dots = collect(0, dots)
     w_relay(depth - 1, groups[3])
     for k in range(1, depth - 1):
-        collect(k)
+        dots = collect(k, dots)
     multiply(depth - 1)
-    collect(depth - 1)
-
+    dots = collect(depth - 1, dots)
+
+    scale_in = inverse[:, 0:1]
+    pull = scale_in * scale_in * scale_in * (dots / model)
     for j in range(depth):
-        for source in range(4):
-            at = (4 * j + source) * shard
-            out_ref[:, at : at + shard] = y_in[j, source]
+        block = scale_in * norm_cut[j] - x_cut[j].astype(jnp.float32) * pull
+        token[:, j * width : (j + 1) * width] = block.astype(token.dtype)
+
+    start = jnp.int32(0)
+    for frame in range(owner_ref.shape[0]):
+        start = start + jnp.where(owner_ref[frame] == me, 2 * frame, 0)
+    one, two = order_ref[2 * me], order_ref[2 * me + 1]
+    keep_first = (one == start) | (one == start + 1)
+    leading = jnp.where(keep_first, one, two) == start
+    sending[...] = jnp.where(keep_first, token[half:rows], token[0:half])
+    frame_recv = copies.slots(1)
+    copies.send(sending, received, frame_recv, core)
+    store_token = pltpu.make_async_copy(token, token_ref, load_sem.at[10])
+    store_token.start()
+    load_p.wait()
+    kept = jnp.where(keep_first, token[0:half], token[half:rows])
+    copies.wait(received, frame_recv, core)
+    other = received[...]
+    frame = jnp.concatenate(
+        [jnp.where(leading, kept, other), jnp.where(leading, other, kept)], axis=0
+    )
+    post = lax.dot_general(
+        frame, project[...], (((1,), (1,)), ((), ())), preferred_element_type=jnp.float32
+    )
+    post = post * post_in[...].reshape(1, post.shape[1])
+    flat = normed[...]
+    post = (
+        post
+        - jnp.mean(post, axis=1, keepdims=True)
+        - flat * jnp.mean(post * flat, axis=1, keepdims=True)
+    )
+    encoder[...] = (deviation[:, 0:1] * post).astype(encoder.dtype)
+    store_encoder = pltpu.make_async_copy(encoder, encoder_ref.at[0], load_sem.at[11])
+    store_encoder.start()
     copies.drain()
     counts.append((copies.sends, copies.recvs))
+    store_token.wait()
+    store_encoder.wait()
 
 
 def layer_grads(arguments, count):
-    order, mask, queries, out_grad, row_delta, keys, values, weight = arguments
+    (
+        order,
+        mask,
+        queries,
+        out_grad,
+        row_delta,
+        keys,
+        values,
+        weight,
+        layer_input,
+        norm_gain,
+        frame_owner,
+        features,
+        post_gain,
+        projector,
+    ) = arguments
     depth = count // 4
     rows = queries.shape[0]
     half = rows // 2
@@ -598,10 +700,15 @@
     def build(counts, sends, recvs):
         return pl.pallas_call(
         functools.partial(layer_kernel, depth, counts),
-        out_shape=jax.ShapeDtypeStruct((rows, count * shard), low),
-        in_specs=[smem, smem] + [anywhere] * 6,
-        out_specs=vmem,
+        out_shape=(
+            jax.ShapeDtypeStruct(layer_input.shape, low),
+            jax.ShapeDtypeStruct(features.shape, low),
+        ),
+        in_specs=[smem, smem] + [anywhere] * 7 + [anywhere, smem, anywhere, anywhere, anywhere],
+        out_specs=(anywhere, anywhere),
         scratch_shapes=[
+            pltpu.VMEM(norm_gain.shape, wide),
+            pltpu.VMEM(post_gain.shape, wide),
             pltpu.VMEM((2, rows, HD), low),
             pltpu.VMEM(kv_shape, low),
             pltpu.VMEM(kv_shape, low),
@@ -627,7 +734,20 @@
             pltpu.VMEM((2, 2, 2, rows, 2 * HD), low),
             pltpu.VMEM((depth, 2, 2, rows, shard), low),
             pltpu.VMEM((depth, 4, rows, shard), low),
-            pltpu.SemaphoreType.DMA((13,)),
+            pltpu.VMEM(layer_input.shape, low),
+            pltpu.VMEM((depth, rows, 4 * shard), low),
+            pltpu.VMEM((depth, 8, 4 * shard), wide),
+            pltpu.VMEM((rows, 128), wide),
+            pltpu.VMEM((depth, rows, 4 * shard), wide),
+            pltpu.VMEM(layer_input.shape, low),
+            pltpu.VMEM((half, layer_input.shape[1]), low),
+            pltpu.VMEM((half, layer_input.shape[1]), low),
+            pltpu.VMEM(features.shape[1:], low),
+            pltpu.VMEM(features.shape[1:], wide),
+            pltpu.VMEM((rows, 128), wide),
+            pltpu.VMEM(projector.shape, low),
+            pltpu.VMEM(features.shape[1:], low),
+            pltpu.SemaphoreType.DMA((15,)),
             pltpu.SemaphoreType.DMA((sends,)),
             pltpu.SemaphoreType.DMA((recvs,)),
         ],
@@ -640,10 +760,6 @@
     counts = []
     jax.eval_shape(build(counts, 4096, 4096), *arguments)
     return build([], *counts[0])(*arguments)
-
-
-def swapped(array, axis, apart):
-    return lax.ppermute(array, axis, [(i, i ^ 1 << apart) for i in range(lax.axis_size(axis))])
 
 
 def body(
@@ -671,47 +787,14 @@
         keys,
         values,
         qkv_weight,
+        layer_input,
+        norm_gain,
+        frame_owner,
+        vision_features,
+        post_gain,
+        projector,
     )
-    tok_rows = queries.shape[0]
-    half_len = tok_rows // 2
-    my_index = lax.axis_index("seq")
-    my_blocks = lax.dynamic_slice_in_dim(block_order, 2 * my_index, 2, 0)
-    norm_grad = layer_grads(arguments, lax.axis_size("seq"))
-    inputs = layer_input.astype(jnp.float32)
-    inverse = lax.rsqrt(jnp.mean(inputs * inputs, axis=1, keepdims=True) + EPSILON)
-    scaled = norm_grad.astype(jnp.float32) * norm_gain
-    token_grad = (
-        inverse * scaled - inputs * inverse**3 * jnp.mean(scaled * inputs, axis=1, keepdims=True)
-    ).astype(jnp.bfloat16)
-    frame_table = jnp.arange(frame_owner.shape[0], dtype=jnp.int32)
-    my_frame = jnp.sum(jnp.where(frame_owner == my_index, frame_table, 0))
-    keep_first = my_blocks[0] // 2 == my_frame
-    kept_block = jnp.where(keep_first, my_blocks[0], my_blocks[1])
-    leading = kept_block % 2 == 0
-    halves = token_grad.reshape(2, half_len, token_grad.shape[1])
-    kept = jnp.where(keep_first, halves[0], halves[1])
-    sending = jnp.where(keep_first, halves[1], halves[0])
-    received = swapped(sending, "seq", 0)
-    frame_rows = jnp.where(
-        leading,
-        jnp.concatenate([kept, received], axis=0),
-        jnp.concatenate([received, kept], axis=0),
-    )
-    post_grad = jnp.dot(frame_rows, projector.T, preferred_element_type=jnp.float32)
-    features = vision_features[0].astype(jnp.float32)
-    centered = features - jnp.mean(features, axis=1, keepdims=True)
-    deviation = lax.rsqrt(jnp.mean(centered * centered, axis=1, keepdims=True) + EPSILON)
-    normed = centered * deviation
-    weighted = post_grad * post_gain
-    encoder_grad = (
-        deviation
-        * (
-            weighted
-            - jnp.mean(weighted, axis=1, keepdims=True)
-            - normed * jnp.mean(weighted * normed, axis=1, keepdims=True)
-        )
-    ).astype(jnp.bfloat16)
-    return (token_grad, encoder_grad[None])
+    return layer_grads(arguments, lax.axis_size("seq"))
 
 
 def solution(mesh):

time: 94.4 us -> 85.2 us (0.903)
  matrix products: 6.14 us -> 0 us
  other arithmetic: 5.43 us -> 0 us
  Pallas kernels: 75.6 us -> 80.4 us
  between operations: 5.13 us -> 0.64 us
  local copies, waits for them, and re-layouts: 1.35 us -> 3.86 us
    dot_general x1 -> x0, matrix products: 6.14 us -> none  [body(): jnp.dot(frame_rows, projector.T, preferred_element_type=jnp.float32)]
    pallas_call x1, Pallas kernels: 75.6 us -> 80.4 us  [layer_grads(): return build([], *counts[0])(*arguments)]
    unnamed x12 -> x2, local copies, waits for them, and re-layouts: 0.04 us -> 3.86 us
    reduce_sum x4 -> x0, other arithmetic: 3.75 us -> none  [the longest x1 2.1 us: body(): jnp.mean(inputs * inputs, axis=1, keepdims=True) + EPSILON]
    broadcast_in_dim x1 -> x0, other arithmetic: 0.95 us -> none  [body(): return (token_grad, encoder_grad[None])]
  transfers between devices with their start and end apart: 1 -> 0, of which waited for: 0 -> 0; matrix products, arithmetic and copies ran while one was open for 0% -> 0% of each run, Pallas kernels for 0% -> 0%
where the time goes in v3:
time: 85.2 us; the launch traced here: 84.9 us
  Pallas kernels  80.4 us (94%)
  local copies, waits for them, and re-layouts  3.86 us (5%)
    pallas_call x1, Pallas kernels, layer_grads(): return build([], *counts[0])(*arguments)  80.4 us
    unnamed x2, local copies, waits for them, and re-layouts  3.86 us

profile of v3, /device:TPU:0, one launch (start us, length us, event | category | flops | bytes accessed | tf_op | source)
XLA Modules:
  0.0 84.9 jit_solution(11873479787222684222)
XLA Ops:
  0.6 80.4 %layer_grads.1 = (bf16[128,3584]{1,0:T(8,128)(2,1)}, bf16[1,128,1152]{2,1,0:T(8,128)(2,1)}) custom-call(s32[32]{0:T(128)} %order_ref.1, s32[32,32]{1,0:T(8,128)} %mask_ref.1, bf16[128,1792]{1,0:T(8,128)(2,1)} %queries_ref.1, bf16[128,1792]{1,0:T(8,128)(2,1)} %grads_ref.1, f32[14,128]{1,0:T(8,128)} %bitcast.1, bf16[128,256]{1,0:T(8,128)(2,1)} %keys_ref.1, ...), custom_call_target="tpu_custom_call" | custom-call | tf_op jit(solution)/shard_map/layer_grads/pallas_call | solution.py:762
  81.1 2.2 %copy.18 = bf16[128,3584]{1,0:T(8,128)(2,1)} copy(bf16[128,3584]{1,0:T(8,128)(2,1)} %get-tuple-element.4) | data formatting | bytes 1835008
  83.3 1.7 %copy.19 = bf16[1,128,1152]{2,1,0:T(8,128)(2,1)} copy(bf16[1,128,1152]{2,1,0:T(8,128)(2,1)} %get-tuple-element.5) | data formatting | bytes 589824

commit v4 on v3

--- a/solution.py
+++ b/solution.py
@@ -16,6 +16,7 @@
 EPSILON = 1e-06
 NEGATIVE = -1e30
 PIECES = 4
+CUTS = 4
 MESH = pl.DeviceIdType.MESH
 
 
@@ -667,6 +668,41 @@
     counts.append((copies.sends, copies.recvs))
     store_token.wait()
     store_encoder.wait()
+
+
+def hand_over_kernel(token_ref, encoder_ref, token_out, encoder_out, token, encoder, sem):
+    rows = token.shape[0] // CUTS
+    moves = [
+        (token_ref.at[at], token_out.at[at], token.at[at])
+        for at in (pl.ds(i * rows, rows) for i in range(CUTS))
+    ] + [(encoder_ref, encoder_out, encoder)]
+    loads, stores = [], []
+    for i, (source, target, buffer) in enumerate(moves):
+        loads.append(pltpu.make_async_copy(source, buffer, sem.at[0, i]))
+        stores.append(pltpu.make_async_copy(buffer, target, sem.at[1, i]))
+    for copy in loads:
+        copy.start()
+    for copy_in, copy_out in zip(loads, stores):
+        copy_in.wait()
+        copy_out.start()
+    for copy in stores:
+        copy.wait()
+
+
+def hand_over(token, encoder):
+    anywhere = pl.BlockSpec(memory_space=pl.ANY)
+    return pl.pallas_call(
+        hand_over_kernel,
+        out_shape=tuple(jax.ShapeDtypeStruct(a.shape, a.dtype) for a in (token, encoder)),
+        in_specs=[anywhere, anywhere],
+        out_specs=(anywhere, anywhere),
+        scratch_shapes=[
+            pltpu.VMEM(token.shape, token.dtype),
+            pltpu.VMEM(encoder.shape, encoder.dtype),
+            pltpu.SemaphoreType.DMA((2, CUTS + 1)),
+        ],
+        name="hand_over",
+    )(token, encoder)
 
 
 def layer_grads(arguments, count):
@@ -794,7 +830,7 @@
         post_gain,
         projector,
     )
-    return layer_grads(arguments, lax.axis_size("seq"))
+    return hand_over(*layer_grads(arguments, lax.axis_size("seq")))
 
 
 def solution(mesh):

time: 85.2 us -> 83.5 us (0.980)
  local copies, waits for them, and re-layouts: 3.86 us -> 0 us
  Pallas kernels: 80.4 us -> 82.6 us
    unnamed x2 -> x0, local copies, waits for them, and re-layouts: 3.86 us -> none
    pallas_call x0 -> x1, Pallas kernels: none -> 2.17 us  [hand_over(): pl.pallas_call(hand_over_kernel, out_shape=tuple((jax.ShapeDtypeStruct(a....]
where the time goes in v4:
time: 83.5 us; the launch traced here: 83.3 us
  Pallas kernels  82.6 us (99%)
    pallas_call x1, Pallas kernels, layer_grads(): return build([], *counts[0])(*arguments)  80.4 us
    pallas_call x1, Pallas kernels, hand_over(): pl.pallas_call(hand_over_kernel, out_shape=tuple((jax.ShapeDtypeStruct(a....  2.17 us

profile of v4, /device:TPU:0, one launch (start us, length us, event | category | flops | bytes accessed | tf_op | source)
XLA Modules:
  0.0 83.3 jit_solution(13452881817220858465)
XLA Ops:
  0.6 80.4 %layer_grads.1 = (bf16[128,3584]{1,0:T(8,128)(2,1)}, bf16[1,128,1152]{2,1,0:T(8,128)(2,1)}) custom-call(s32[32]{0:T(128)} %order_ref.1, s32[32,32]{1,0:T(8,128)} %mask_ref.1, bf16[128,1792]{1,0:T(8,128)(2,1)} %queries_ref.1, bf16[128,1792]{1,0:T(8,128)(2,1)} %grads_ref.1, f32[14,128]{1,0:T(8,128)} %bitcast.1, bf16[128,256]{1,0:T(8,128)(2,1)} %keys_ref.1, ...), custom_call_target="tpu_custom_call" | custom-call | tf_op jit(solution)/shard_map/layer_grads/pallas_call | solution.py:798
  81.1 2.2 %hand_over.1 = (bf16[128,3584]{1,0:T(8,128)(2,1)}, bf16[1,128,1152]{2,1,0:T(8,128)(2,1)}) custom-call(bf16[128,3584]{1,0:T(8,128)(2,1)} %get-tuple-element.4.token_ref, bf16[1,128,1152]{2,1,0:T(8,128)(2,1)} %get-tuple-element.5.encoder_ref), custom_call_target="tpu_custom_call" | custom-call | tf_op jit(solution)/shard_map/hand_over/pallas_call | solution.py:694
